TPU v7x, 8 devices: a whole 2x2x1 slice. The times are simulated.
8 devices in a mesh: node: 2 (over z, y), data: 4 (over x, core).
Axes of the slice: x: 2, y: 2, z: 1, core: 2. Of those that a mesh axis runs over, the one named last changes fastest.
Arguments:
- tokens: bfloat16 [65536, 768], P(('node', 'data'))
- grad_out: bfloat16 [65536, 768], P(('node', 'data'))
- weights: bfloat16 [8, 768, 768], replicated
- a_old: float32 [8, 768, 768], replicated
- s_old: float32 [8, 768, 768], replicated
- a_inv: float32 [8, 768, 768], replicated
- s_inv: float32 [8, 768, 768], replicated
Outputs:
- output 1: float32 [8, 768, 768], replicated
- output 2: float32 [8, 768, 768], replicated
- output 3: float32 [8, 768, 768], replicated
All inputs are finite; a program needn't handle non-finite values.
Results may differ from a plain program's by a relative error of at most 0.00149.
Values are sent between devices in bfloat16 or wider.
A program may use at most 1 GiB of HBM per device.

v0:
```python
import jax
import jax.numpy as jnp
from jax import lax
from jax.sharding import PartitionSpec as P, NamedSharding

FACTOR_DECAY = 0.8
GELU_SCALE = 0.7978845608028654
GELU_CUBIC = 0.044715


def gelu_value(pre_act):
    pre_f = pre_act.astype(jnp.float32)
    return 0.5 * pre_f * (1.0 + jnp.tanh(GELU_SCALE * (pre_f + GELU_CUBIC * pre_f * pre_f * pre_f)))


def gelu_slope(pre_act):
    pre_f = pre_act.astype(jnp.float32)
    tanh_val = jnp.tanh(GELU_SCALE * (pre_f + GELU_CUBIC * pre_f * pre_f * pre_f))
    return 0.5 * (1.0 + tanh_val) + 0.5 * pre_f * (1.0 - tanh_val * tanh_val) * GELU_SCALE * (1.0 + 3.0 * GELU_CUBIC * pre_f * pre_f)


def row_gram(left, right):
    return lax.dot_general(left, right, (((0,), (0,)), ((), ())), preferred_element_type=jnp.float32)


def local_terms(tok_rows, dout_rows, weights, inv_total):
    layers = weights.shape[0]
    hidden = [tok_rows]
    pre_list = []
    for layer in range(layers - 1):
        pre_act = jnp.dot(hidden[layer], weights[layer], preferred_element_type=jnp.float32).astype(jnp.bfloat16)
        pre_list.append(pre_act)
        hidden.append(gelu_value(pre_act).astype(jnp.bfloat16))
    w_parts = [None] * layers
    a_parts = [None] * layers
    s_parts = [None] * layers
    grad_h = dout_rows
    for layer in reversed(range(layers)):
        if layer == layers - 1:
            grad_pre = grad_h
        else:
            grad_pre = (grad_h.astype(jnp.float32) * gelu_slope(pre_list[layer])).astype(jnp.bfloat16)
        w_parts[layer] = row_gram(hidden[layer], grad_pre) * inv_total
        a_parts[layer] = row_gram(hidden[layer], hidden[layer]) * inv_total
        s_parts[layer] = row_gram(grad_pre, grad_pre) * inv_total
        if layer > 0:
            grad_h = lax.dot_general(grad_pre, weights[layer], (((1,), (1,)), ((), ())), preferred_element_type=jnp.float32).astype(jnp.bfloat16)
    return jnp.stack(w_parts), jnp.stack(a_parts), jnp.stack(s_parts)


def finish(grad_w, a_cur, s_cur, a_old, s_old, a_inv, s_inv):
    a_new = FACTOR_DECAY * a_old + (1.0 - FACTOR_DECAY) * a_cur
    s_new = FACTOR_DECAY * s_old + (1.0 - FACTOR_DECAY) * s_cur
    left = jnp.einsum('lij,ljk->lik', a_inv, grad_w, precision=lax.Precision.HIGHEST, preferred_element_type=jnp.float32)
    update = jnp.einsum('lij,ljk->lik', left, s_inv, precision=lax.Precision.HIGHEST, preferred_element_type=jnp.float32)
    return update, a_new, s_new


def solution(mesh):
    batch_axes = ('node', 'data')
    row_spec = P(batch_axes, None)
    full_spec = P()

    def kfac_step(tokens, grad_out, weights, a_old, s_old, a_inv, s_inv):
        inv_total = 1.0 / tokens.shape[0]

        def per_device(tok_rows, dout_rows, layer_w, a_prev, s_prev, a_pre, s_pre):
            w_loc, a_loc, s_loc = local_terms(tok_rows, dout_rows, layer_w, inv_total)
            grad_w, a_cur, s_cur = lax.psum((w_loc, a_loc, s_loc), batch_axes)
            return finish(grad_w, a_cur, s_cur, a_prev, s_prev, a_pre, s_pre)

        return jax.shard_map(per_device, mesh=mesh, in_specs=(row_spec, row_spec, full_spec, full_spec, full_spec, full_spec, full_spec), out_specs=(full_spec, full_spec, full_spec), check_vma=False)(tokens, grad_out, weights, a_old, s_old, a_inv, s_inv)

    return kfac_step
```

profile of v0, /device:TPU:0, one launch (start us, length us, event | category | flops | bytes accessed | tf_op | source)
XLA Modules:
  0.0 1713.1 jit_solution(4290935208606389956)
XLA Ops:
  23.3 21.7 %convolution_convert_fusion.11 = bf16[8192,768]{1,0:T(8,128)(2,1)} fusion(bf16[8,768,768]{2,1,0:T(8,128)(2,1)S(1)} %copy-done, bf16[8192,768]{1,0:T(8,128)(2,1)} %convolution_convert_fusion.12), kind=kOutput, calls=%fused_computation.139 | convolution fusion | flops 9732882432 | bytes 26345472 | tf_op jit(solution)/shard_map/dot_general | solution.py:31
  45.0 22.0 %convolution_convert_fusion.10 = bf16[8192,768]{1,0:T(8,128)(2,1)} fusion(bf16[8,768,768]{2,1,0:T(8,128)(2,1)S(1)} %copy-done, bf16[8192,768]{1,0:T(8,128)(2,1)} %convolution_convert_fusion.11), kind=kOutput, calls=%fused_computation.138 | convolution fusion | flops 9732882432 | bytes 26345472 | tf_op jit(solution)/shard_map/dot_general | solution.py:31
  67.1 21.6 %convolution_convert_fusion.9 = bf16[8192,768]{1,0:T(8,128)(2,1)} fusion(bf16[8,768,768]{2,1,0:T(8,128)(2,1)S(1)} %copy-done, bf16[8192,768]{1,0:T(8,128)(2,1)} %convolution_convert_fusion.10), kind=kOutput, calls=%fused_computation.137 | convolution fusion | flops 9732882432 | bytes 26345472 | tf_op jit(solution)/shard_map/dot_general | solution.py:31
  88.7 21.6 %convolution_convert_fusion.8 = bf16[8192,768]{1,0:T(8,128)(2,1)} fusion(bf16[8,768,768]{2,1,0:T(8,128)(2,1)S(1)} %copy-done, bf16[8192,768]{1,0:T(8,128)(2,1)} %convolution_convert_fusion.9), kind=kOutput, calls=%fused_computation.136 | convolution fusion | flops 9732882432 | bytes 26345472 | tf_op jit(solution)/shard_map/dot_general | solution.py:31
  110.3 21.7 %convolution_convert_fusion.7 = bf16[8192,768]{1,0:T(8,128)(2,1)} fusion(bf16[8,768,768]{2,1,0:T(8,128)(2,1)S(1)} %copy-done, bf16[8192,768]{1,0:T(8,128)(2,1)} %convolution_convert_fusion.8), kind=kOutput, calls=%fused_computation.135 | convolution fusion | flops 9732882432 | bytes 26345472 | tf_op jit(solution)/shard_map/dot_general | solution.py:31
  131.9 21.9 %convolution_convert_fusion.6 = bf16[8192,768]{1,0:T(8,128)(2,1)} fusion(bf16[8,768,768]{2,1,0:T(8,128)(2,1)S(1)} %copy-done, bf16[8192,768]{1,0:T(8,128)(2,1)} %convolution_convert_fusion.7), kind=kOutput, calls=%fused_computation.134 | convolution fusion | flops 9732882432 | bytes 26345472 | tf_op jit(solution)/shard_map/dot_general | solution.py:31
  153.8 28.5 %fusion.18 = bf16[8192,768]{1,0:T(8,128)(2,1)} fusion(bf16[8192,768]{1,0:T(8,128)(2,1)} %convolution_convert_fusion.6, bf16[8192,768]{1,0:T(8,128)(2,1)} %param.8, bf16[8,768,768]{2,1,0:T(8,128)(2,1)S(1)} %copy-done), kind=kOutput, calls=%fused_computation.67 | convolution fusion | flops 9802088448 | bytes 38928384 | tf_op jit(solution)/shard_map/dot_general | solution.py:47
  182.3 28.6 %fusion.25 = bf16[8192,768]{1,0:T(8,128)(2,1)} fusion(bf16[8192,768]{1,0:T(8,128)(2,1)} %convolution_convert_fusion.7, bf16[8192,768]{1,0:T(8,128)(2,1)} %fusion.18, bf16[8,768,768]{2,1,0:T(8,128)(2,1)S(1)} %copy-done), kind=kOutput, calls=%fused_computation.74 | convolution fusion | flops 9802088448 | bytes 38928384 | tf_op jit(solution)/shard_map/dot_general | solution.py:47
  210.9 28.6 %fusion.31 = bf16[8192,768]{1,0:T(8,128)(2,1)} fusion(bf16[8192,768]{1,0:T(8,128)(2,1)} %convolution_convert_fusion.8, bf16[8192,768]{1,0:T(8,128)(2,1)} %fusion.25, bf16[8,768,768]{2,1,0:T(8,128)(2,1)S(1)} %copy-done), kind=kOutput, calls=%fused_computation.80 | convolution fusion | flops 9802088448 | bytes 38928384 | tf_op jit(solution)/shard_map/dot_general | solution.py:47
  239.5 28.8 %fusion.37 = bf16[8192,768]{1,0:T(8,128)(2,1)} fusion(bf16[8192,768]{1,0:T(8,128)(2,1)} %convolution_convert_fusion.9, bf16[8192,768]{1,0:T(8,128)(2,1)} %fusion.31, bf16[8,768,768]{2,1,0:T(8,128)(2,1)S(1)} %copy-done), kind=kOutput, calls=%fused_computation.86 | convolution fusion | flops 9802088448 | bytes 38928384 | tf_op jit(solution)/shard_map/dot_general | solution.py:47
  268.3 28.5 %fusion.43 = bf16[8192,768]{1,0:T(8,128)(2,1)} fusion(bf16[8192,768]{1,0:T(8,128)(2,1)} %convolution_convert_fusion.10, bf16[8192,768]{1,0:T(8,128)(2,1)} %fusion.37, bf16[8,768,768]{2,1,0:T(8,128)(2,1)S(1)} %copy-done), kind=kOutput, calls=%fused_computation.92 | convolution fusion | flops 9802088448 | bytes 38928384 | tf_op jit(solution)/shard_map/dot_general | solution.py:47
  296.8 29.1 %fusion.49 = bf16[8192,768]{1,0:T(8,128)(2,1)} fusion(bf16[8192,768]{1,0:T(8,128)(2,1)} %convolution_convert_fusion.11, bf16[8192,768]{1,0:T(8,128)(2,1)} %fusion.43, bf16[8,768,768]{2,1,0:T(8,128)(2,1)} %param.9), kind=kOutput, calls=%fused_computation.98 | convolution fusion | flops 9802088448 | bytes 38928384 | tf_op jit(solution)/shard_map/dot_general | solution.py:47
  325.9 29.1 %fusion.55 = bf16[8192,768]{1,0:T(8,128)(2,1)} fusion(bf16[8192,768]{1,0:T(8,128)(2,1)} %convolution_convert_fusion.12, bf16[8192,768]{1,0:T(8,128)(2,1)} %fusion.49, bf16[8,768,768]{2,1,0:T(8,128)(2,1)} %param.9), kind=kOutput, calls=%fused_computation.104 | convolution fusion | flops 9802088448 | bytes 38928384 | tf_op jit(solution)/shard_map/dot_general | solution.py:47
  355.0 20.3 %bitcast_dynamic-update-slice_fusion.8 = f32[8,768,768]{1,2,0:T(8,128)} fusion(bf16[8192,768]{1,0:T(8,128)(2,1)} %fusion.55), kind=kOutput, calls=%fused_computation.150 | convolution fusion | flops 9664266240 | bytes 27525120 | tf_op jit(solution)/shard_map/dot_general | solution.py:23
  524.5 26.2 %bitcast_dynamic-update-slice_fusion.23 = f32[8,768,768]{1,2,0:T(8,128)} fusion(f32[8,768,768]{1,2,0:T(8,128)} %bitcast_dynamic-update-slice_fusion, bf16[8192,768]{1,0:T(8,128)(2,1)} %fusion.49, bf16[8192,768]{1,0:T(8,128)(2,1)} %convolution_convert_fusion.12), kind=kOutput, calls=%fused_computation.165 | convolution fusion | flops 9727180800 | bytes 27525120 | tf_op jit(solution)/shard_map/dot_general | solution.py:23
  550.7 26.3 %bitcast_dynamic-update-slice_fusion.22 = f32[8,768,768]{1,2,0:T(8,128)} fusion(f32[8,768,768]{1,2,0:T(8,128)} %bitcast_dynamic-update-slice_fusion.23, bf16[8192,768]{1,0:T(8,128)(2,1)} %fusion.43, bf16[8192,768]{1,0:T(8,128)(2,1)} %convolution_convert_fusion.11), kind=kOutput, calls=%fused_computation.164 | convolution fusion | flops 9727180800 | bytes 27525120 | tf_op jit(solution)/shard_map/dot_general | solution.py:23
  577.0 26.5 %bitcast_dynamic-update-slice_fusion.21 = f32[8,768,768]{1,2,0:T(8,128)} fusion(f32[8,768,768]{1,2,0:T(8,128)} %bitcast_dynamic-update-slice_fusion.22, bf16[8192,768]{1,0:T(8,128)(2,1)} %fusion.37, bf16[8192,768]{1,0:T(8,128)(2,1)} %convolution_convert_fusion.10), kind=kOutput, calls=%fused_computation.163 | convolution fusion | flops 9727180800 | bytes 27525120 | tf_op jit(solution)/shard_map/dot_general | solution.py:23
  603.5 26.3 %bitcast_dynamic-update-slice_fusion.20 = f32[8,768,768]{1,2,0:T(8,128)} fusion(f32[8,768,768]{1,2,0:T(8,128)} %bitcast_dynamic-update-slice_fusion.21, bf16[8192,768]{1,0:T(8,128)(2,1)} %fusion.31, bf16[8192,768]{1,0:T(8,128)(2,1)} %convolution_convert_fusion.9), kind=kOutput, calls=%fused_computation.162 | convolution fusion | flops 9727180800 | bytes 27525120 | tf_op jit(solution)/shard_map/dot_general | solution.py:23
  629.8 26.2 %bitcast_dynamic-update-slice_fusion.19 = f32[8,768,768]{1,2,0:T(8,128)} fusion(f32[8,768,768]{1,2,0:T(8,128)} %bitcast_dynamic-update-slice_fusion.20, bf16[8192,768]{1,0:T(8,128)(2,1)} %fusion.25, bf16[8192,768]{1,0:T(8,128)(2,1)} %convolution_convert_fusion.8), kind=kOutput, calls=%fused_computation.161 | convolution fusion | flops 9727180800 | bytes 27525120 | tf_op jit(solution)/shard_map/dot_general | solution.py:23
  656.0 26.3 %bitcast_dynamic-update-slice_fusion.18 = f32[8,768,768]{1,2,0:T(8,128)} fusion(f32[8,768,768]{1,2,0:T(8,128)} %bitcast_dynamic-update-slice_fusion.19, bf16[8192,768]{1,0:T(8,128)(2,1)} %fusion.18, bf16[8192,768]{1,0:T(8,128)(2,1)} %convolution_convert_fusion.7), kind=kOutput, calls=%fused_computation.160 | convolution fusion | flops 9727180800 | bytes 27525120 | tf_op jit(solution)/shard_map/dot_general | solution.py:23
  682.3 26.5 %bitcast_dynamic-update-slice_fusion.17 = f32[8,768,768]{1,2,0:T(8,128)} fusion(f32[8,768,768]{1,2,0:T(8,128)} %bitcast_dynamic-update-slice_fusion.18, bf16[8192,768]{1,0:T(8,128)(2,1)} %param.8, bf16[8192,768]{1,0:T(8,128)(2,1)} %convolution_convert_fusion.6), kind=kOutput, calls=%fused_computation.159 | convolution fusion | flops 9727180800 | bytes 27525120 | tf_op jit(solution)/shard_map/dot_general | solution.py:23
  708.8 26.8 %bitcast_dynamic-update-slice_fusion.15 = f32[8,768,768]{1,2,0:T(8,128)} fusion(f32[8,768,768]{1,2,0:T(8,128)} %bitcast_dynamic-update-slice_fusion.16, bf16[8192,768]{1,0:T(8,128)(2,1)} %convolution_convert_fusion.12), kind=kOutput, calls=%fused_computation.157 | convolution fusion | flops 9727180800 | bytes 14942208 | tf_op jit(solution)/shard_map/dot_general | solution.py:23
  735.6 27.1 %bitcast_dynamic-update-slice_fusion.14 = f32[8,768,768]{1,2,0:T(8,128)} fusion(f32[8,768,768]{1,2,0:T(8,128)} %bitcast_dynamic-update-slice_fusion.15, bf16[8192,768]{1,0:T(8,128)(2,1)} %convolution_convert_fusion.11), kind=kOutput, calls=%fused_computation.156 | convolution fusion | flops 9727180800 | bytes 14942208 | tf_op jit(solution)/shard_map/dot_general | solution.py:23
  762.8 26.0 %bitcast_dynamic-update-slice_fusion.13 = f32[8,768,768]{1,2,0:T(8,128)} fusion(f32[8,768,768]{1,2,0:T(8,128)} %bitcast_dynamic-update-slice_fusion.14, bf16[8192,768]{1,0:T(8,128)(2,1)S(1)} %bitcast.140), kind=kOutput, calls=%fused_computation.155 | convolution fusion | flops 9727180800 | bytes 14942208 | tf_op jit(solution)/shard_map/dot_general | solution.py:23
  788.8 26.0 %bitcast_dynamic-update-slice_fusion.12 = f32[8,768,768]{1,2,0:T(8,128)} fusion(f32[8,768,768]{1,2,0:T(8,128)} %bitcast_dynamic-update-slice_fusion.13, bf16[8192,768]{1,0:T(8,128)(2,1)S(1)} %bitcast.138), kind=kOutput, calls=%fused_computation.154 | convolution fusion | flops 9727180800 | bytes 14942208 | tf_op jit(solution)/shard_map/dot_general | solution.py:23
  814.9 26.0 %bitcast_dynamic-update-slice_fusion.11 = f32[8,768,768]{1,2,0:T(8,128)} fusion(f32[8,768,768]{1,2,0:T(8,128)} %bitcast_dynamic-update-slice_fusion.12, bf16[8192,768]{1,0:T(8,128)(2,1)S(1)} %bitcast.136), kind=kOutput, calls=%fused_computation.153 | convolution fusion | flops 9727180800 | bytes 14942208 | tf_op jit(solution)/shard_map/dot_general | solution.py:23
  840.9 26.0 %bitcast_dynamic-update-slice_fusion.10 = f32[8,768,768]{1,2,0:T(8,128)} fusion(f32[8,768,768]{1,2,0:T(8,128)} %bitcast_dynamic-update-slice_fusion.11, bf16[8192,768]{1,0:T(8,128)(2,1)S(1)} %bitcast.134), kind=kOutput, calls=%fused_computation.152 | convolution fusion | flops 9727180800 | bytes 14942208 | tf_op jit(solution)/shard_map/dot_general | solution.py:23
  866.9 26.0 %bitcast_dynamic-update-slice_fusion.9 = f32[8,768,768]{1,2,0:T(8,128)} fusion(f32[8,768,768]{1,2,0:T(8,128)} %bitcast_dynamic-update-slice_fusion.10, bf16[8192,768]{1,0:T(8,128)(2,1)S(1)} %bitcast.132), kind=kOutput, calls=%fused_computation.151 | convolution fusion | flops 9727180800 | bytes 14942208 | tf_op jit(solution)/shard_map/dot_general | solution.py:23
  930.7 597.9 %all-reduce.3.cloned.1.call-done = (f32[8,768,768]{1,2,0:T(8,128)}, f32[8,768,768]{1,2,0:T(8,128)}, f32[8,768,768]{1,2,0:T(8,128)}) async-done(((f32[8,768,768]{1,2,0:T(8,128)}, f32[8,768,768]{1,2,0:T(8,128)}, f32[8,768,768]{1,2,0:T(8,128)}), (f32[8,768,768]{1,2,0:T(8,128)}, f32[8,768,768]{1,2,0:T(8,128)}, f32[8,768,768]{1,2,0:T(8,128)})) %all-reduce.3.cloned.1.call-update) | async-done | bytes 56623120 | tf_op jit(solution)/shard_map/psum | solution.py:69
  1528.5 37.8 %multiply_add_fusion = (f32[8,768,768]{1,2,0:T(8,128)}, f32[8,768,768]{1,2,0:T(8,128)}) fusion(f32[8,768,768]{1,2,0:T(8,128)} %get-tuple-element.8, f32[8,768,768]{1,2,0:T(8,128)} %copy.27, f32[8,768,768]{1,2,0:T(8,128)} %get-tuple-element.7, f32[8,768,768]{1,2,0:T(8,128)} %copy.18), kind=kLoop, calls=%fused_computation.126 | loop fusion | flops 28311552 | bytes 113246208 | tf_op jit(solution)/shard_map/add | solution.py:53
  1603.6 51.2 %fusion.125 = f32[8,768,768]{1,2,0:T(8,128)S(1)} fusion(f32[8,768,768]{1,2,0:T(8,128)} %get-tuple-element.6, f32[8,768,768]{2,1,0:T(8,128)} %param.12), kind=kOutput, calls=%fused_computation.194 | convolution fusion | flops 43486543872 | bytes 56623104 | tf_op jit(solution)/shard_map/lij,ljk->lik/dot_general | solution.py:54
  1654.8 51.3 %fusion.126 = f32[8,768,768]{2,1,0:T(8,128)} fusion(f32[8,768,768]{1,2,0:T(8,128)S(1)} %fusion.125, f32[8,768,768]{2,1,0:T(8,128)} %param.13), kind=kOutput, calls=%fused_computation.195 | convolution fusion | flops 43486543872 | bytes 56623104 | tf_op jit(solution)/shard_map/lij,ljk->lik/dot_general | solution.py:55
  (74 shorter events, 240.4 us)
Async XLA Ops:
  7.2 1521.4 %all-reduce.3.cloned.1.call-start = ((), (), s32[]{:S(2)}) async-start(), calls=%async_computation | async-start | bytes 113246208 | tf_op jit(solution)/shard_map/psum | solution.py:69
  7.2 16.1 copy-start
  296.8 78.4 %slice-start = ((s8[12582912]{0:T(1024)(128)(4,1)}), s8[4194304]{0:T(1024)(128)(4,1)S(1)}, s32[]{:S(2)}) async-start(s8[12582912]{0:T(1024)(128)(4,1)} %bitcast.125), calls=%async_computation.1 | async-start | bytes 8388608
  296.8 78.4 %slice-start.1 = ((s8[12582912]{0:T(1024)(128)(4,1)}), s8[4194304]{0:T(1024)(128)(4,1)S(1)}, s32[]{:S(2)}) async-start(s8[12582912]{0:T(1024)(128)(4,1)} %bitcast.125), calls=%async_computation.2 | async-start | bytes 8388608
  325.9 49.4 %slice-start.2 = ((s8[12582912]{0:T(1024)(128)(4,1)}), s8[4194304]{0:T(1024)(128)(4,1)S(1)}, s32[]{:S(2)}) async-start(s8[12582912]{0:T(1024)(128)(4,1)} %bitcast.125), calls=%async_computation.3 | async-start | bytes 8388608
  420.7 40.2 %slice-start.6 = ((s8[12582912]{0:T(1024)(128)(4,1)}), s8[4194304]{0:T(1024)(128)(4,1)S(1)}, s32[]{:S(2)}) async-start(s8[12582912]{0:T(1024)(128)(4,1)} %bitcast.129), calls=%async_computation.7 | async-start | bytes 8388608
  420.7 40.2 %slice-start.7 = ((s8[12582912]{0:T(1024)(128)(4,1)}), s8[4194304]{0:T(1024)(128)(4,1)S(1)}, s32[]{:S(2)}) async-start(s8[12582912]{0:T(1024)(128)(4,1)} %bitcast.129), calls=%async_computation.8 | async-start | bytes 8388608
  440.8 20.1 %slice-start.8 = ((s8[12582912]{0:T(1024)(128)(4,1)}), s8[4194304]{0:T(1024)(128)(4,1)S(1)}, s32[]{:S(2)}) async-start(s8[12582912]{0:T(1024)(128)(4,1)} %bitcast.129), calls=%async_computation.9 | async-start | bytes 8388608
  472.5 40.4 %slice-start.3 = ((s8[12582912]{0:T(1024)(128)(4,1)}), s8[4194304]{0:T(1024)(128)(4,1)S(1)}, s32[]{:S(2)}) async-start(s8[12582912]{0:T(1024)(128)(4,1)} %bitcast.127), calls=%async_computation.4 | async-start | bytes 8388608
  472.5 40.5 %slice-start.4 = ((s8[12582912]{0:T(1024)(128)(4,1)}), s8[4194304]{0:T(1024)(128)(4,1)S(1)}, s32[]{:S(2)}) async-start(s8[12582912]{0:T(1024)(128)(4,1)} %bitcast.127), calls=%async_computation.5 | async-start | bytes 8388608
  492.8 20.2 %slice-start.5 = ((s8[12582912]{0:T(1024)(128)(4,1)}), s8[4194304]{0:T(1024)(128)(4,1)S(1)}, s32[]{:S(2)}) async-start(s8[12582912]{0:T(1024)(128)(4,1)} %bitcast.127), calls=%async_computation.6 | async-start | bytes 8388608
  708.8 53.9 %slice-start.21 = ((s8[12582912]{0:T(1024)(128)(4,1)}), s8[4194304]{0:T(1024)(128)(4,1)S(1)}, s32[]{:S(2)}) async-start(s8[12582912]{0:T(1024)(128)(4,1)} %bitcast.139), calls=%async_computation.22 | async-start | bytes 8388608
  708.8 53.9 %slice-start.22 = ((s8[12582912]{0:T(1024)(128)(4,1)}), s8[4194304]{0:T(1024)(128)(4,1)S(1)}, s32[]{:S(2)}) async-start(s8[12582912]{0:T(1024)(128)(4,1)} %bitcast.139), calls=%async_computation.23 | async-start | bytes 8388608
  735.6 27.1 %slice-start.23 = ((s8[12582912]{0:T(1024)(128)(4,1)}), s8[4194304]{0:T(1024)(128)(4,1)S(1)}, s32[]{:S(2)}) async-start(s8[12582912]{0:T(1024)(128)(4,1)} %bitcast.139), calls=%async_computation.24 | async-start | bytes 8388608
  735.6 53.2 %slice-start.18 = ((s8[12582912]{0:T(1024)(128)(4,1)}), s8[4194304]{0:T(1024)(128)(4,1)S(1)}, s32[]{:S(2)}) async-start(s8[12582912]{0:T(1024)(128)(4,1)} %bitcast.137), calls=%async_computation.19 | async-start | bytes 8388608
  735.6 53.2 %slice-start.19 = ((s8[12582912]{0:T(1024)(128)(4,1)}), s8[4194304]{0:T(1024)(128)(4,1)S(1)}, s32[]{:S(2)}) async-start(s8[12582912]{0:T(1024)(128)(4,1)} %bitcast.137), calls=%async_computation.20 | async-start | bytes 8388608
  762.7 26.0 %slice-start.20 = ((s8[12582912]{0:T(1024)(128)(4,1)}), s8[4194304]{0:T(1024)(128)(4,1)S(1)}, s32[]{:S(2)}) async-start(s8[12582912]{0:T(1024)(128)(4,1)} %bitcast.137), calls=%async_computation.21 | async-start | bytes 8388608
  762.7 52.1 %slice-start.15 = ((s8[12582912]{0:T(1024)(128)(4,1)}), s8[4194304]{0:T(1024)(128)(4,1)S(1)}, s32[]{:S(2)}) async-start(s8[12582912]{0:T(1024)(128)(4,1)} %bitcast.135), calls=%async_computation.16 | async-start | bytes 8388608
  762.7 52.1 %slice-start.16 = ((s8[12582912]{0:T(1024)(128)(4,1)}), s8[4194304]{0:T(1024)(128)(4,1)S(1)}, s32[]{:S(2)}) async-start(s8[12582912]{0:T(1024)(128)(4,1)} %bitcast.135), calls=%async_computation.17 | async-start | bytes 8388608
  788.8 26.0 %slice-start.17 = ((s8[12582912]{0:T(1024)(128)(4,1)}), s8[4194304]{0:T(1024)(128)(4,1)S(1)}, s32[]{:S(2)}) async-start(s8[12582912]{0:T(1024)(128)(4,1)} %bitcast.135), calls=%async_computation.18 | async-start | bytes 8388608
  788.8 52.1 %slice-start.12 = ((s8[12582912]{0:T(1024)(128)(4,1)}), s8[4194304]{0:T(1024)(128)(4,1)S(1)}, s32[]{:S(2)}) async-start(s8[12582912]{0:T(1024)(128)(4,1)} %bitcast.133), calls=%async_computation.13 | async-start | bytes 8388608
  788.8 52.1 %slice-start.13 = ((s8[12582912]{0:T(1024)(128)(4,1)}), s8[4194304]{0:T(1024)(128)(4,1)S(1)}, s32[]{:S(2)}) async-start(s8[12582912]{0:T(1024)(128)(4,1)} %bitcast.133), calls=%async_computation.14 | async-start | bytes 8388608
  814.8 26.0 %slice-start.14 = ((s8[12582912]{0:T(1024)(128)(4,1)}), s8[4194304]{0:T(1024)(128)(4,1)S(1)}, s32[]{:S(2)}) async-start(s8[12582912]{0:T(1024)(128)(4,1)} %bitcast.133), calls=%async_computation.15 | async-start | bytes 8388608
  814.8 52.1 %slice-start.9 = ((s8[12582912]{0:T(1024)(128)(4,1)}), s8[4194304]{0:T(1024)(128)(4,1)S(1)}, s32[]{:S(2)}) async-start(s8[12582912]{0:T(1024)(128)(4,1)} %bitcast.131), calls=%async_computation.10 | async-start | bytes 8388608
  814.8 52.0 %slice-start.10 = ((s8[12582912]{0:T(1024)(128)(4,1)}), s8[4194304]{0:T(1024)(128)(4,1)S(1)}, s32[]{:S(2)}) async-start(s8[12582912]{0:T(1024)(128)(4,1)} %bitcast.131), calls=%async_computation.11 | async-start | bytes 8388608
  840.9 26.0 %slice-start.11 = ((s8[12582912]{0:T(1024)(128)(4,1)}), s8[4194304]{0:T(1024)(128)(4,1)S(1)}, s32[]{:S(2)}) async-start(s8[12582912]{0:T(1024)(128)(4,1)} %bitcast.131), calls=%async_computation.12 | async-start | bytes 8388608
Sparse Core Ops, SparseCore 0:
  893.1 635.4 all-reduce.2
where the time goes:
time: 1720 us; the launch traced here: 1710 us
  matrix products  988 us (57%)
  waiting for transfers between devices  598 us (35%)
  local copies, waits for them, and re-layouts  75.1 us (4%)
  other arithmetic  37.8 us (2%)
    psum x1, waiting for transfers between devices, per_device(): grad_w, a_cur, s_cur = lax.psum((w_loc, a_loc, s_loc), batch_axes)  598 us
    dot_general x24, matrix products, row_gram(): lax.dot_general(left, right, (((0,), (0,)), ((), ())), preferred_element_...  538 us
    dot_general x7, matrix products, local_terms(): lax.dot_general(grad_pre, weights[layer], (((1,), (1,)), ((), ())), prefe...  201 us
    dot_general x7, matrix products, local_terms(): jnp.dot(hidden[layer], weights[layer], preferred_element_type=jnp.float32)  147 us
    unnamed x54, local copies, waits for them, and re-layouts  75.1 us
    dot_general x1, matrix products, finish(): jnp.einsum('lij,ljk->lik', left, s_inv, precision=lax.Precision.HIGHEST,...  51.3 us
    dot_general x1, matrix products, finish(): jnp.einsum('lij,ljk->lik', a_inv, grad_w, precision=lax.Precision.HIGHEST...  51.2 us
    add x1, other arithmetic, finish(): s_new = FACTOR_DECAY * s_old + (1.0 - FACTOR_DECAY) * s_cur  37.8 us
  transfers between devices with their start and end apart: 1, of which 1 were waited for; matrix products, arithmetic and copies ran while one was open for 2% of the time, Pallas kernels for 0%

commit v1 on v0

v1 whole, which is shorter than its diff:
```python
import functools
import jax
import jax.numpy as jnp
from jax import lax
from jax.experimental import pallas as pl
from jax.experimental.pallas import tpu as pltpu
from jax.sharding import PartitionSpec as P

FACTOR_DECAY = 0.8
GELU_SCALE = 0.7978845608028654
GELU_CUBIC = 0.044715
D = 768
B = 256
TILE = 1024
SUB = 256


def tn(left, right):
    return lax.dot_general(left, right, (((0,), (0,)), ((), ())), preferred_element_type=jnp.float32)


def nt(left, right):
    return lax.dot_general(left, right, (((1,), (1,)), ((), ())), preferred_element_type=jnp.float32)


def gelu_parts(pre_act):
    z = pre_act.astype(jnp.float32)
    q = (GELU_CUBIC * z) * z
    gz = GELU_SCALE * z
    t = jnp.tanh(gz + gz * q)
    hz = 0.5 * z
    return q, t, hz


def gelu_value(pre_act):
    _, t, hz = gelu_parts(pre_act)
    return (hz + hz * t).astype(jnp.bfloat16)


def gelu_both(pre_act):
    q, t, hz = gelu_parts(pre_act)
    slope = (0.5 + 0.5 * t) + (hz * (1.0 - t * t)) * (GELU_SCALE + (3.0 * GELU_SCALE) * q)
    return (hz + hz * t).astype(jnp.bfloat16), slope


def gram_add(acc, x):
    acc[0:B, :] += tn(x[:, 0:B], x)
    acc[B:2 * B, 0:2 * B] += tn(x[:, B:2 * B], x[:, B:])
    acc[B:2 * B, 2 * B:] += tn(x[:, 2 * B:], x[:, 2 * B:])


def fwd_kernel(n_tiles, layers, tok_ref, w_ref, z_ref, a_ref, h_s):
    l = pl.program_id(0)
    t = pl.program_id(1)

    @pl.when(l == 0)
    def _():
        h_s[t] = tok_ref[...]

    @pl.when(t == 0)
    def _():
        a_ref[...] = jnp.zeros_like(a_ref)

    @pl.when(l < layers - 1)
    def _():
        x = h_s[t]
        for r in range(0, TILE, SUB):
            for c in range(0, D, B):
                z = jnp.dot(x[r:r + SUB, :], w_ref[0, :, c:c + B], preferred_element_type=jnp.float32).astype(jnp.bfloat16)
                z_ref[0, r:r + SUB, c:c + B] = z
                h_s[t, r:r + SUB, c:c + B] = gelu_value(z)
        gram_add(a_ref.at[0], x)

    @pl.when(l == layers - 1)
    def _():
        gram_add(a_ref.at[0], h_s[t])


def bwd_kernel(n_tiles, first, count, dout_ref, z_ref, tok_ref, w_ref, s_ref, g_ref, gout_ref, g_s):
    i = pl.program_id(0)
    t = pl.program_id(1)

    @pl.when(i == 0)
    def _():
        g_s[t] = dout_ref[...]

    @pl.when(t == 0)
    def _():
        s_ref[...] = jnp.zeros_like(s_ref)
        g_ref[...] = jnp.zeros_like(g_ref)

    def inner():
        g = g_s[t]
        z = z_ref[0]
        h, slope = gelu_both(z)
        for r in range(0, TILE, SUB):
            for c in range(0, D, B):
                dh = nt(g[r:r + SUB, :], w_ref[0, c:c + B, :]).astype(jnp.bfloat16)
                g_s[t, r:r + SUB, c:c + B] = (dh.astype(jnp.float32) * slope[r:r + SUB, c:c + B]).astype(jnp.bfloat16)
        for m in range(0, D, B):
            g_ref[0, m:m + B, :] += tn(g[:, m:m + B], h)
        gram_add(s_ref.at[0], g)
        gout_ref[...] = g_s[t]

    def last():
        g = g_s[t]
        h = tok_ref[...]
        for m in range(0, D, B):
            g_ref[0, m:m + B, :] += tn(g[:, m:m + B], h)
        gram_add(s_ref.at[0], g)
        gout_ref[...] = g

    final = first - (count - 1) == 0
    if final:
        pl.when(i < count - 1)(inner)
        pl.when(i == count - 1)(last)
    else:
        inner()


def forward(tok, w):
    n, d = tok.shape
    layers = w.shape[0]
    nt_ = n // TILE
    z_map = lambda l, t: (jnp.minimum(l, layers - 2), jnp.where(l < layers - 1, t, nt_ - 1), 0)
    return pl.pallas_call(
        functools.partial(fwd_kernel, nt_, layers),
        grid=(layers, nt_),
        in_specs=[
            pl.BlockSpec((TILE, d), lambda l, t: (jnp.where(l == 0, t, nt_ - 1), 0)),
            pl.BlockSpec((1, d, d), lambda l, t: (jnp.minimum(l, layers - 2), 0, 0)),
        ],
        out_specs=[
            pl.BlockSpec((1, TILE, d), z_map),
            pl.BlockSpec((1, 2 * B, d), lambda l, t: (l, 0, 0)),
        ],
        out_shape=[
            jax.ShapeDtypeStruct((layers - 1, n, d), jnp.bfloat16),
            jax.ShapeDtypeStruct((layers, 2 * B, d), jnp.float32),
        ],
        scratch_shapes=[pltpu.VMEM((nt_, TILE, d), jnp.bfloat16)],
        compiler_params=pltpu.CompilerParams(vmem_limit_bytes=60 * 2 ** 20),
        cost_estimate=pl.CostEstimate(flops=int(layers * 2 * n * d * d * 1.6), bytes_accessed=100 * 2 ** 20, transcendentals=0),
        name="fwd_stack",
    )(tok, w)


def backward(dout, z, tok, w, first, count):
    n, d = tok.shape
    nt_ = n // TILE
    lay = lambda i: first - i
    return pl.pallas_call(
        functools.partial(bwd_kernel, nt_, first, count),
        grid=(count, nt_),
        in_specs=[
            pl.BlockSpec((TILE, d), lambda i, t: (jnp.where(i == 0, t, nt_ - 1), 0)),
            pl.BlockSpec((1, TILE, d), lambda i, t: (jnp.maximum(lay(i) - 1, 0), jnp.where(lay(i) > 0, t, nt_ - 1), 0)),
            pl.BlockSpec((TILE, d), lambda i, t: (jnp.where(lay(i) == 0, t, 0), 0)),
            pl.BlockSpec((1, d, d), lambda i, t: (lay(i), 0, 0)),
        ],
        out_specs=[
            pl.BlockSpec((1, 2 * B, d), lambda i, t: (i, 0, 0)),
            pl.BlockSpec((1, d, d), lambda i, t: (i, 0, 0)),
            pl.BlockSpec((TILE, d), lambda i, t: (jnp.where(i == count - 1, t, 0), 0)),
        ],
        out_shape=[
            jax.ShapeDtypeStruct((count, 2 * B, d), jnp.float32),
            jax.ShapeDtypeStruct((count, d, d), jnp.float32),
            jax.ShapeDtypeStruct((n, d), jnp.bfloat16),
        ],
        scratch_shapes=[pltpu.VMEM((nt_, TILE, d), jnp.bfloat16)],
        compiler_params=pltpu.CompilerParams(vmem_limit_bytes=60 * 2 ** 20),
        cost_estimate=pl.CostEstimate(flops=int(count * 2 * n * d * d * 2.7), bytes_accessed=100 * 2 ** 20, transcendentals=0),
        name="bwd_stack",
    )(dout, z, tok, w)


def unpack(p):
    b00, b01, b02 = p[:, 0:B, 0:B], p[:, 0:B, B:2 * B], p[:, 0:B, 2 * B:]
    b11, b12, b22 = p[:, B:, 0:B], p[:, B:, B:2 * B], p[:, B:, 2 * B:]
    tr = lambda x: jnp.swapaxes(x, 1, 2)
    return jnp.concatenate([
        jnp.concatenate([b00, b01, b02], 2),
        jnp.concatenate([tr(b01), b11, b12], 2),
        jnp.concatenate([tr(b02), tr(b12), b22], 2)], 1)


CHUNKS = ((7, 2), (5, 2), (3, 2), (1, 2))


def solution(mesh):
    batch_axes = ('node', 'data')
    row_spec = P(batch_axes, None)
    full_spec = P()

    def kfac_step(tokens, grad_out, weights, a_old, s_old, a_inv, s_inv):
        inv_total = 1.0 / tokens.shape[0]

        def per_device(tok, dout, w, a_prev, s_prev, a_pre, s_pre):
            z, a_loc = forward(tok, w)
            a_sum = lax.psum(a_loc, batch_axes)
            s_list, g_list = [], []
            g = dout
            for first, count in CHUNKS:
                s_loc, g_loc, g = backward(g, z, tok, w, first, count)
                s_sum, g_sum = lax.psum((s_loc, g_loc), batch_axes)
                s_list.append(s_sum[::-1])
                g_list.append(g_sum[::-1])
            s_sum = jnp.concatenate(s_list[::-1], 0)
            gt_sum = jnp.concatenate(g_list[::-1], 0) * inv_total
            a_new = FACTOR_DECAY * a_prev + (1.0 - FACTOR_DECAY) * (unpack(a_sum) * inv_total)
            s_new = FACTOR_DECAY * s_prev + (1.0 - FACTOR_DECAY) * (unpack(s_sum) * inv_total)
            me = lax.axis_index('node') * lax.axis_size('data') + lax.axis_index('data')
            take = lambda x: lax.dynamic_slice_in_dim(x, me, 1, 0)[0]
            hi = lax.Precision.HIGHEST
            left = lax.dot_general(take(a_pre), take(gt_sum), (((1,), (1,)), ((), ())), precision=hi, preferred_element_type=jnp.float32)
            upd = jnp.dot(left, take(s_pre), precision=hi, preferred_element_type=jnp.float32)
            update = lax.all_gather(upd, batch_axes)
            return update, a_new, s_new

        return jax.shard_map(per_device, mesh=mesh, in_specs=(row_spec, row_spec, full_spec, full_spec, full_spec, full_spec, full_spec), out_specs=(full_spec, full_spec, full_spec), check_vma=False)(tokens, grad_out, weights, a_old, s_old, a_inv, s_inv)

    return kfac_step
```

time: 1720 us -> 1170 us (0.68)
  matrix products: 988 us -> 18.6 us
  Pallas kernels: 0 us -> 493 us
  waiting for transfers between devices: 598 us -> 509 us
    dot_general x40 -> x2, matrix products: 988 us -> 18.6 us  [the longest x1 9.67 us: per_device(): lax.dot_general(take(a_pre), take(gt_sum), (((1,), (1,)), ((), ())), prec...]
    pallas_call x0 -> x5, Pallas kernels: none -> 493 us  [the longest x4 322 us: backward(): pl.pallas_call(functools.partial(bwd_kernel, nt_, first, count), grid=(co...]
    psum x1, waiting for transfers between devices: 598 us -> 501 us  [per_device(): s_sum, g_sum = lax.psum((s_loc, g_loc), batch_axes)]
    unnamed x54 -> x22, local copies, waits for them, and re-layouts: 75.1 us -> 28.7 us
    rev x0 -> x8, local copies, waits for them, and re-layouts: none -> 27.3 us  [the longest x4 19.9 us: per_device(): g_list.append(g_sum[::-1])]
    slice x0 -> x6, local copies, waits for them, and re-layouts: none -> 26.8 us  [the longest x4 19.7 us: unpack(): b00, b01, b02 = (p[:, 0:B, 0:B], p[:, 0:B, B:2 * B], p[:, 0:B, 2 * B:])]
  transfers between devices with their start and end apart: 1 -> 2, of which waited for: 1 -> 2; matrix products, arithmetic and copies ran while one was open for 2% -> 7% of each run, Pallas kernels for 0% -> 0%
where the time goes in v1:
time: 1170 us; the launch traced here: 1160 us
  waiting for transfers between devices  509 us (44%)
  Pallas kernels  493 us (42%)
  local copies, waits for them, and re-layouts  88.9 us (8%)
  other arithmetic  36.8 us (3%)
  matrix products  18.6 us (2%)
  between operations  14.6 us (1%)
    psum x1, waiting for transfers between devices, per_device(): s_sum, g_sum = lax.psum((s_loc, g_loc), batch_axes)  501 us
    pallas_call x4, Pallas kernels, backward(): pl.pallas_call(functools.partial(bwd_kernel, nt_, first, count), grid=(co...  322 us
    pallas_call x1, Pallas kernels, forward(): pl.pallas_call(functools.partial(fwd_kernel, nt_, layers), grid=(layers,...  171 us
    add x1, other arithmetic, per_device(): FACTOR_DECAY * a_prev + (1.0 - FACTOR_DECAY) * (unpack(a_sum) * inv_total)  36.8 us
    unnamed x22, local copies, waits for them, and re-layouts  28.7 us
  transfers between devices with their start and end apart: 2, of which 2 were waited for; matrix products, arithmetic and copies ran while one was open for 7% of the time, Pallas kernels for 0%

profile of v1, /device:TPU:0, one launch (start us, length us, event | category | flops | bytes accessed | tf_op | source)
XLA Modules:
  0.0 1160.5 jit_solution(9825968897692419440)
XLA Ops:
  7.2 170.6 %fwd_stack.1 = (bf16[7,8192,768]{2,1,0:T(8,128)(2,1)}, f32[8,512,768]{2,1,0:T(8,128)}) custom-call(bf16[8192,768]{1,0:T(8,128)(2,1)} %tok_ref.9, bf16[8,768,768]{2,1,0:T(8,128)(2,1)} %w_ref.9), custom_call_target="tpu_custom_call" | custom-call | flops 123695054848 | bytes 104857600 | tf_op jit(solution)/shard_map/fwd_stack/pallas_call | solution.py:126
  177.8 85.4 %bwd_stack.4 = (f32[2,512,768]{2,1,0:T(8,128)}, f32[2,768,768]{2,1,0:T(8,128)}, bf16[8192,768]{1,0:T(8,128)(2,1)}) custom-call(bf16[8192,768]{1,0:T(8,128)(2,1)} %dout_ref.1, bf16[7,8192,768]{2,1,0:T(8,128)(2,1)} %get-tuple-element.16.z_ref, bf16[8192,768]{1,0:T(8,128)(2,1)} %tok_ref.9, bf16[8,768,768]{2,1,0:T(8,128)(2,1)} %w_ref.9), custom_call_target="tpu_custom_call" | custom-call | flops 52183851008 | bytes 104857600 | tf_op jit(solution)/shard_map/bwd_stack/pallas_call | solution.py:152
  263.1 85.6 %bwd_stack.5 = (f32[2,512,768]{2,1,0:T(8,128)}, f32[2,768,768]{2,1,0:T(8,128)}, bf16[8192,768]{1,0:T(8,128)(2,1)}) custom-call(bf16[8192,768]{1,0:T(8,128)(2,1)} %get-tuple-element.17.dout_ref, bf16[7,8192,768]{2,1,0:T(8,128)(2,1)} %get-tuple-element.16.z_ref, bf16[8192,768]{1,0:T(8,128)(2,1)} %tok_ref.9, bf16[8,768,768]{2,1,0:T(8,128)(2,1)} %w_ref.9), custom_call_target="tpu_custom_call" | custom-call | flops 52183851008 | bytes 104857600 | tf_op jit(solution)/shard_map/bwd_stack/pallas_call | solution.py:152
  348.7 85.3 %bwd_stack.6 = (f32[2,512,768]{2,1,0:T(8,128)}, f32[2,768,768]{2,1,0:T(8,128)}, bf16[8192,768]{1,0:T(8,128)(2,1)}) custom-call(bf16[8192,768]{1,0:T(8,128)(2,1)} %get-tuple-element.18.dout_ref, bf16[7,8192,768]{2,1,0:T(8,128)(2,1)} %get-tuple-element.16.z_ref, bf16[8192,768]{1,0:T(8,128)(2,1)} %tok_ref.9, bf16[8,768,768]{2,1,0:T(8,128)(2,1)} %w_ref.9), custom_call_target="tpu_custom_call" | custom-call | flops 52183851008 | bytes 104857600 | tf_op jit(solution)/shard_map/bwd_stack/pallas_call | solution.py:152
  434.0 66.1 %bwd_stack.7 = (f32[2,512,768]{2,1,0:T(8,128)}, f32[2,768,768]{2,1,0:T(8,128)}, bf16[8192,768]{1,0:T(8,128)(2,1)}) custom-call(bf16[8192,768]{1,0:T(8,128)(2,1)} %get-tuple-element.19.dout_ref, bf16[7,8192,768]{2,1,0:T(8,128)(2,1)} %get-tuple-element.16.z_ref, bf16[8192,768]{1,0:T(8,128)(2,1)} %tok_ref.9, bf16[8,768,768]{2,1,0:T(8,128)(2,1)} %w_ref.9), custom_call_target="tpu_custom_call" | custom-call | flops 52183851008 | bytes 104857600 | tf_op jit(solution)/shard_map/bwd_stack/pallas_call | solution.py:152
  500.1 5.0 rev.24
  505.1 1.9 rev.28
  507.0 5.0 rev.25
  511.9 1.9 rev.29
  513.8 4.9 rev.26
  518.7 1.8 rev.30
  520.5 5.0 rev.27
  525.5 1.9 rev.31
  527.5 501.0 %all-reduce.3.cloned.1.call-done = (f32[2,768,768]{2,1,0:T(8,128)}, f32[2,768,768]{2,1,0:T(8,128)}, f32[2,768,768]{2,1,0:T(8,128)}, f32[2,768,768]{2,1,0:T(8,128...) async-done(((f32[2,768,768]{2,1,0:T(8,128)}, f32[2,768,768]{2,1,0:T(8,128)}, ...) | async-done | bytes 44040208 | tf_op jit(solution)/shard_map/psum | solution.py:206
  1028.5 9.7 fusion.7
  1038.2 9.0 fusion.9
  1047.2 2.2 constant_dynamic-update-slice_fusion.3
  1052.6 3.2 slice.58
  1055.8 2.5 slice.60
  1058.3 5.9 slice.52
  1064.2 4.6 slice.54
  1068.8 3.5 fusion.19
  1072.4 1.9 copy.17
  1074.3 2.9 copy.18
  1077.2 3.2 copy.19
  1080.4 7.1 fusion.20
  1087.4 2.9 copy.16
  1090.3 2.9 copy.11
  1093.2 2.9 copy.12
  1096.1 36.8 %fusion = (f32[8,768,768]{2,1,0:T(8,128)}, f32[8,768,768]{2,1,0:T(8,128)}) fusion(f32[8,256,256]{2,1,0:T(8,128)} %get-tuple-element.43, f32[8,256,256]{2,1,0:T(8,128)} %copy.12, f32[8,256,256]{2,1,0:T(8,128)} %copy.11, f32[8,256,512]{2,1,0:T(8,128)} %slice.54, f32[8,256,256]{2,1,0:T(8,128)} %bitcast.23, f32[8,256,768]{2,1,0:T(8,128)} %slice.52, ...), kind=kLoop, calls=%fused_computation.5 | loop fusion | flops 75497472 | bytes 113246208 | tf_op jit(solution)/shard_map/add | solution.py:211
  1132.9 7.6 all-gather.3.cloned.1.call-done
  1140.5 12.7 %copy.33 = f32[8,768,768]{2,1,0:T(8,128)} copy(f32[8,768,768]{2,1,0:T(8,128)} %bitcast.19) | data formatting | bytes 37748736
  (21 shorter events, 3.3 us)
Async XLA Ops:
  7.2 1021.4 %all-reduce.3.cloned.1.call-start = ((), (), s32[]{:S(2)}) async-start(), calls=%async_computation.1 | async-start | bytes 88080384 | tf_op jit(solution)/shard_map/psum | solution.py:206
  500.1 5.0 copy-start.6
  507.0 5.0 copy-start.5
  513.8 4.9 copy-start.4
  520.5 5.0 copy-start.3
  527.4 613.1 %all-gather.3.cloned.1.call-start = ((), (), s32[]{:S(2)}) async-start(), calls=%async_computation | async-start | bytes 21233664 | tf_op jit(solution)/shard_map/all_gather | solution.py:218
  1047.2 2.8 copy-start.2
  1049.4 2.0 copy-start.1
  1050.2 2.2 copy-start
Sparse Core Ops, SparseCore 0:
  527.5 500.9 all-reduce.2
  1047.3 93.1 all-gather.2

commit v2 on v0

v2 whole, which is shorter than its diff:
```python
import functools
import jax
import jax.numpy as jnp
from jax import lax
from jax.experimental import pallas as pl
from jax.experimental.pallas import tpu as pltpu
from jax.sharding import PartitionSpec as P

FACTOR_DECAY = 0.8
GELU_SCALE = 0.7978845608028654
GELU_CUBIC = 0.044715
D = 768
B = 256
NT = 8
DEV = 8
AR = 64
GR = 96
SR = AR + GR
L = 8
MESH = pl.DeviceIdType.MESH
T1, T2, T3, T4, T5, T6, T7 = 0, 1, 5, 7, 1, 5, 7


def tn(left, right):
    return lax.dot_general(left, right, (((0,), (0,)), ((), ())), preferred_element_type=jnp.float32)


def nt(left, right):
    return lax.dot_general(left, right, (((1,), (1,)), ((), ())), preferred_element_type=jnp.float32)


def half_parts(half_act):
    y = half_act.astype(jnp.float32)
    sq = jnp.minimum(y * y, 1e37)
    kp = (8.0 * GELU_SCALE * GELU_CUBIC) * sq
    a = 2.0 * GELU_SCALE + kp
    return y, kp, a, jnp.tanh(y * a)


def gelu_value(half_act):
    y, _, _, t = half_parts(half_act)
    return (y + y * t).astype(jnp.bfloat16)


def gelu_both(half_act):
    y, kp, a, t = half_parts(half_act)
    opt = 1.0 + t
    h = y * opt
    slope2 = opt + (h * (1.0 - t)) * ((a + kp) + kp)
    return h.astype(jnp.bfloat16), slope2


def add_rows(acc, p, base, rows, first, c0, val):
    n = val.shape[0]
    r = first
    while r < first + n:
        d, o = divmod(r, rows)
        k = min(rows - o, first + n - r)
        acc[p, d, base + o:base + o + k, c0:c0 + val.shape[1]] += val[r - first:r - first + k, :]
        r += k


def gram_add(acc, p, x):
    add_rows(acc, p, 0, AR, 0, 0, tn(x[:, 0:B], x))
    add_rows(acc, p, 0, AR, B, 0, tn(x[:, B:2 * B], x[:, B:]))
    add_rows(acc, p, 0, AR, B, 2 * B, tn(x[:, 2 * B:], x[:, 2 * B:]))


def split3(x):
    hi = x.astype(jnp.bfloat16)
    r = x - hi.astype(jnp.float32)
    mid = r.astype(jnp.bfloat16)
    lo = (r - mid.astype(jnp.float32)).astype(jnp.bfloat16)
    return hi, mid, lo


def step_kernel(tile, inv_total, tok, dout, w_ref, ainv, y_hbm, a_out, g_out,
                buf, hbuf, ybuf, wh, acc, r1, r2a, r2b, r3a, r3b, own, ainv_v,
                ssem, rsem, lsem, tsem, ysem, asem):
    w = pl.program_id(0)
    t = pl.program_id(1)
    node = lax.axis_index('node')
    data = lax.axis_index('data')
    cy, cx, cc = node, data // 2, lax.rem(data, 2)
    partner = (cy, cx * 2 + 1 - cc)
    xn = (cy, (1 - cx) * 2 + cc)
    yn = (1 - cy, cx * 2 + cc)
    me = cy * 4 + cx * 2 + cc

    def chunk(yy, xx, c):
        return yy * 4 + xx * 2 + c

    @pl.when((w == 0) & (t == 0))
    def _():
        bar = pltpu.get_barrier_semaphore()
        for dev in (partner, xn, yn):
            pl.semaphore_signal(bar, inc=1, device_id=dev, device_id_type=MESH)
        pl.semaphore_wait(bar, 3)
        for i in range(NT):
            pltpu.make_async_copy(tok.at[pl.ds(i * tile, tile), :], buf.at[0, i], tsem.at[i]).start()

    def rcopy(src, dst, p, k, dev):
        return pltpu.make_async_remote_copy(src_ref=src, dst_ref=dst, send_sem=ssem.at[p, k], recv_sem=rsem.at[p, k],
                                            device_id=dev, device_id_type=MESH)

    def stages(rows, out, idx1, idx2, p1, p2, bwd):
        hh = rows // 2

        def c1(p):
            return [rcopy(acc.at[p, chunk(i // 2, i % 2, 1 - cc), pl.ds(0, rows)], r1.at[p, i, pl.ds(0, rows)], p, i, partner)
                    for i in range(4)]

        def c2(p):
            a = [rcopy(acc.at[p, chunk(i, 1 - cx, cc), pl.ds(0, hh)], r2a.at[p, i, pl.ds(0, hh)], p, 4 + i, xn) for i in range(2)]
            b = [rcopy(acc.at[p, chunk(1 - cy, i, cc), pl.ds(hh, hh)], r2b.at[p, i, pl.ds(0, hh)], p, 6 + i, yn) for i in range(2)]
            return a + b

        def c3(p):
            return [rcopy(acc.at[p, chunk(1 - cy, cx, cc), pl.ds(0, hh)], r3a.at[p, pl.ds(0, hh)], p, 8, yn),
                    rcopy(acc.at[p, chunk(cy, 1 - cx, cc), pl.ds(hh, hh)], r3b.at[p, pl.ds(0, hh)], p, 9, xn)]

        def c4(p, idx):
            return [rcopy(own.at[p, pl.ds(0, hh)], out.at[idx, me, pl.ds(0, hh)], p, 10, yn),
                    rcopy(own.at[p, pl.ds(hh, hh)], out.at[idx, me, pl.ds(hh, hh)], p, 11, xn)]

        def keep(p, idx):
            return pltpu.make_async_copy(own.at[p, pl.ds(0, rows)], out.at[idx, me], lsem.at[p])

        def c5(p, idx):
            def mv(d, o, k, dev):
                ref = out.at[idx, d, pl.ds(o, hh)]
                return rcopy(ref, ref, p, k, dev)
            a = [mv(chunk(i, cx, cc), 0, 12 + i, xn) for i in range(2)]
            b = [mv(chunk(cy, i, cc), hh, 14 + i, yn) for i in range(2)]
            return a + b

        def c6(p, idx):
            refs = [out.at[idx, chunk(i // 2, i % 2, cc)] for i in range(4)]
            return [rcopy(refs[i], refs[i], p, 16 + i, partner) for i in range(4)]

        def start(cs):
            for c in cs:
                c.start()

        def wait(cs):
            for c in cs:
                c.wait()

        def reduce1():
            start(c1(p1))

        def reduce2():
            wait(c1(p1))
            for i in range(4):
                acc[p1, chunk(i // 2, i % 2, cc), 0:rows, :] += r1[p1, i, 0:rows, :]
            start(c2(p1))

        def reduce3():
            wait(c2(p1))
            for i in range(2):
                acc[p1, chunk(i, cx, cc), 0:hh, :] += r2a[p1, i, 0:hh, :]
                acc[p1, chunk(cy, i, cc), hh:rows, :] += r2b[p1, i, 0:hh, :]
            start(c3(p1))

        def reduce4():
            wait(c3(p1))
            own[p1, 0:hh, :] = (acc[p1, me, 0:hh, :] + r3a[p1, 0:hh, :]) * inv_total
            own[p1, hh:rows, :] = (acc[p1, me, hh:rows, :] + r3b[p1, 0:hh, :]) * inv_total
            if bwd:
                pltpu.make_async_copy(ainv.at[L - 1 - idx1], ainv_v, asem).wait()
                gh, gm, gl = split3(own[p1, AR:SR, :])
                g3 = jnp.concatenate([gh, gm, gl], 0)
                g2 = jnp.concatenate([gh, gm], 0)
                for n in range(0, D, B):
                    ah, am, al = split3(ainv_v[n:n + B, :])
                    d1 = nt(g3, ah)
                    d2 = nt(g2, am)
                    d3 = nt(gh, al)
                    low = (d3 + d2[GR:, :]) + d1[2 * GR:, :]
                    own[p1, AR:SR, n:n + B] = (low + (d2[0:GR, :] + d1[GR:2 * GR, :])) + d1[0:GR, :]
            keep(p1, idx1).start()
            start(c4(p1, idx1))

        def gather5():
            keep(p2, idx2).wait()
            wait(c4(p2, idx2))
            start(c5(p2, idx2))

        def gather6():
            wait(c5(p2, idx2))
            start(c6(p2, idx2))

        def gather7():
            wait(c6(p2, idx2))

        return reduce1, reduce2, reduce3, reduce4, gather5, gather6, gather7

    def at(cond, step, fn):
        pl.when(cond & (t == step))(fn)

    j1, j2 = w - 1, w - 2
    p1, p2 = lax.rem(w + 1, 2), lax.rem(w, 2)
    fw = stages(AR, a_out, j1, j2, p1, p2, False)
    bw = stages(SR, g_out, j1 - L, j2 - L, p1, p2, True)
    red_f = (j1 >= 0) & (j1 < L)
    red_b = (j1 >= L) & (j1 < 2 * L)
    gat_f = (j2 >= 0) & (j2 < L)
    gat_b = (j2 >= L) & (j2 < 2 * L)

    @pl.when(red_b & (t == 0))
    def _():
        pltpu.make_async_copy(ainv.at[L - 1 - (j1 - L)], ainv_v, asem).start()

    for k, (step, rf, rb) in enumerate(((T1, red_f, red_b), (T2, red_f, red_b), (T3, red_f, red_b), (T4, red_f, red_b),
                                        (T5, gat_f, gat_b), (T6, gat_f, gat_b), (T7, gat_f, gat_b))):
        at(rf, step, fw[k])
        at(rb, step, bw[k])

    p = lax.rem(w, 2)
    slot = lax.rem(t, 2)
    half = tile // 2

    @pl.when((t == 0) & (w < 2 * L))
    def _():
        acc[p] = jnp.zeros(acc.shape[1:], jnp.float32)
        wh[...] = w_ref[0] * jnp.bfloat16(0.5)

    @pl.when(w == 0)
    def _():
        pltpu.make_async_copy(tok.at[pl.ds(t * tile, tile), :], buf.at[0, t], tsem.at[t]).wait()

    def put_y(layer, i, s):
        return pltpu.make_async_copy(ybuf.at[s], y_hbm.at[layer, pl.ds(i * tile, tile), :], ysem.at[s])

    def get_y(layer, i, s):
        return pltpu.make_async_copy(y_hbm.at[layer, pl.ds(i * tile, tile), :], ybuf.at[s], ysem.at[s])

    def get_tok(i, s):
        return pltpu.make_async_copy(tok.at[pl.ds(i * tile, tile), :], ybuf.at[s], ysem.at[s])

    @pl.when((w < L) & (w * NT + t >= 2) & (w * NT + t < (L - 1) * NT + 2))
    def _():
        put_y(0, 0, slot).wait()

    @pl.when(w < L - 1)
    def _():
        x = buf.at[p, t]
        for r in range(0, tile, half):
            for c in range(0, D, B):
                y = jnp.dot(x[r:r + half, :], wh[:, c:c + B], preferred_element_type=jnp.float32).astype(jnp.bfloat16)
                ybuf[slot, r:r + half, c:c + B] = y
                buf[1 - p, t, r:r + half, c:c + B] = gelu_value(y)
        gram_add(acc, p, x[...])
        put_y(w, t, slot).start()

    @pl.when(w == L - 1)
    def _():
        @pl.when(t == 0)
        def _():
            for i in range(NT):
                pltpu.make_async_copy(dout.at[pl.ds(i * tile, tile), :], buf.at[0, i], tsem.at[i]).start()
        gram_add(acc, p, buf[p, t])

        @pl.when(t == NT - 1)
        def _():
            get_y(L - 2, 0, 0).start()

    @pl.when(w == L)
    def _():
        pltpu.make_async_copy(dout.at[pl.ds(t * tile, tile), :], buf.at[0, t], tsem.at[t]).wait()

    wn = jnp.where(t == NT - 1, w + 1, w)
    tn_ = jnp.where(t == NT - 1, 0, t + 1)

    @pl.when((w >= L) & (wn < 2 * L - 1))
    def _():
        get_y(2 * L - 2 - wn, tn_, 1 - slot).start()

    @pl.when((w >= L) & (wn == 2 * L - 1))
    def _():
        get_tok(tn_, 1 - slot).start()

    @pl.when((w >= L) & (w < 2 * L))
    def _():
        get_tok(0, slot).wait()

    def grad_add(g, h):
        for m in range(0, D, B):
            add_rows(acc, p, AR, GR, m, 0, tn(g[:, m:m + B], h))

    @pl.when((w >= L) & (w < 2 * L - 1))
    def _():
        g = buf.at[p, t]
        for r in range(0, tile, half):
            for c in range(0, D, B):
                dh = nt(g[r:r + half, :], wh[c:c + B, :]).astype(jnp.bfloat16)
                h, slope2 = gelu_both(ybuf[slot, r:r + half, c:c + B])
                hbuf[r:r + half, c:c + B] = h
                buf[1 - p, t, r:r + half, c:c + B] = (dh.astype(jnp.float32) * slope2).astype(jnp.bfloat16)
        gram_add(acc, p, g[...])
        grad_add(g[...], hbuf[...])

    @pl.when(w == 2 * L - 1)
    def _():
        g = buf[p, t]
        gram_add(acc, p, g)
        grad_add(g, ybuf[slot])


def run_stack(tok, dout, w, a_inv, inv_total):
    n, d = tok.shape
    tile = n // NT
    f32, bf16 = jnp.float32, jnp.bfloat16
    any_spec = pl.BlockSpec(memory_space=pl.ANY)

    def w_map(i, t):
        return (jnp.where(i < L, i, jnp.clip(2 * L - 1 - i, 1, L - 1)), 0, 0)

    return pl.pallas_call(
        functools.partial(step_kernel, tile, inv_total),
        grid=(2 * L + 2, NT),
        in_specs=[any_spec, any_spec, pl.BlockSpec((1, d, d), w_map), any_spec],
        out_specs=[any_spec] * 3,
        out_shape=[
            jax.ShapeDtypeStruct((L - 1, n, d), bf16),
            jax.ShapeDtypeStruct((L, DEV, AR, d), f32),
            jax.ShapeDtypeStruct((L, DEV, SR, d), f32),
        ],
        scratch_shapes=[
            pltpu.VMEM((2, NT, tile, d), bf16),
            pltpu.VMEM((tile, d), bf16),
            pltpu.VMEM((2, tile, d), bf16),
            pltpu.VMEM((d, d), bf16),
            pltpu.VMEM((2, DEV, SR, d), f32),
            pltpu.VMEM((2, 4, SR, d), f32),
            pltpu.VMEM((2, 2, SR // 2, d), f32),
            pltpu.VMEM((2, 2, SR // 2, d), f32),
            pltpu.VMEM((2, SR // 2, d), f32),
            pltpu.VMEM((2, SR // 2, d), f32),
            pltpu.VMEM((2, SR, d), f32),
            pltpu.VMEM((d, d), f32),
            pltpu.SemaphoreType.DMA((2, 20)),
            pltpu.SemaphoreType.DMA((2, 20)),
            pltpu.SemaphoreType.DMA((2,)),
            pltpu.SemaphoreType.DMA((NT,)),
            pltpu.SemaphoreType.DMA((2,)),
            pltpu.SemaphoreType.DMA,
        ],
        compiler_params=pltpu.CompilerParams(vmem_limit_bytes=67043328, collective_id=0, has_side_effects=True),
        cost_estimate=pl.CostEstimate(flops=2 * 33 * n * d * d, bytes_accessed=200 * 2 ** 20, transcendentals=0),
        name="kfac_stack",
    )(tok, dout, w, a_inv)


def finish_kernel(a_ref, g_ref, a_old, s_old, s_inv, upd, a_new, s_new):
    def unfold(p, old, new):
        sc = (1.0 - FACTOR_DECAY)

        def put(r, c, val):
            new[0, r * B:(r + 1) * B, c * B:(c + 1) * B] = FACTOR_DECAY * old[0, r * B:(r + 1) * B, c * B:(c + 1) * B] + sc * val

        for (pr, pc, r, c) in ((0, 0, 0, 0), (0, 1, 0, 1), (0, 2, 0, 2), (1, 0, 1, 1), (1, 1, 1, 2), (1, 2, 2, 2)):
            blk = jnp.concatenate([p[0, d, 0:AR, pc * B:(pc + 1) * B] for d in range(pr * 4, pr * 4 + 4)], 0)
            put(r, c, blk)
            if r != c:
                put(c, r, blk.T)

    unfold(a_ref, a_old, a_new)
    unfold(g_ref, s_old, s_new)
    sh, sm, sl = split3(s_inv[0])
    lt = jnp.concatenate([g_ref[0, d, AR:SR, :] for d in range(DEV)], 0)
    lh, lm, ll = split3(lt)
    for m in range(0, D, B):
        x, y, z = lh[:, m:m + B], lm[:, m:m + B], ll[:, m:m + B]
        low = (tn(y, sm) + tn(x, sl)) + tn(z, sh)
        upd[0, m:m + B, :] = (low + (tn(x, sm) + tn(y, sh))) + tn(x, sh)


def finish(a_red, g_red, a_old, s_old, s_inv):
    f32 = jnp.float32
    full = pl.BlockSpec((1, D, D), lambda l: (l, 0, 0))
    shape = jax.ShapeDtypeStruct((L, D, D), f32)
    return pl.pallas_call(
        finish_kernel,
        grid=(L,),
        in_specs=[
            pl.BlockSpec((1, DEV, AR, D), lambda l: (l, 0, 0, 0)),
            pl.BlockSpec((1, DEV, SR, D), lambda l: (L - 1 - l, 0, 0, 0)),
            full, full, full,
        ],
        out_specs=[full] * 3,
        out_shape=[shape] * 3,
        compiler_params=pltpu.CompilerParams(vmem_limit_bytes=60 * 2 ** 20),
        cost_estimate=pl.CostEstimate(flops=L * 12 * D ** 3, bytes_accessed=160 * 2 ** 20, transcendentals=0),
        name="kfac_finish",
    )(a_red, g_red, a_old, s_old, s_inv)


def solution(mesh):
    batch_axes = ('node', 'data')
    row_spec = P(batch_axes, None)
    full_spec = P()

    def kfac_step(tokens, grad_out, weights, a_old, s_old, a_inv, s_inv):
        inv_total = 1.0 / tokens.shape[0]

        def per_device(tok, dout, w, a_prev, s_prev, a_pre, s_pre):
            _, a_red, g_red = run_stack(tok, dout, w, a_pre, inv_total)
            return tuple(finish(a_red, g_red, a_prev, s_prev, s_pre))

        return jax.shard_map(per_device, mesh=mesh, in_specs=(row_spec, row_spec, full_spec, full_spec, full_spec, full_spec, full_spec), out_specs=(full_spec, full_spec, full_spec), check_vma=False)(tokens, grad_out, weights, a_old, s_old, a_inv, s_inv)

    return kfac_step
```

time: 1720 us -> 821 us (0.48)
  matrix products: 988 us -> 0 us
  Pallas kernels: 0 us -> 820 us
  waiting for transfers between devices: 598 us -> 0 us
  local copies, waits for them, and re-layouts: 75.1 us -> 0 us
  other arithmetic: 37.8 us -> 0 us
    dot_general x40 -> x0, matrix products: 988 us -> none  [the longest x24 538 us: row_gram(): lax.dot_general(left, right, (((0,), (0,)), ((), ())), preferred_element_...]
    pallas_call x0 -> x2, Pallas kernels: none -> 820 us  [the longest x1 760 us: run_stack(): pl.pallas_call(functools.partial(step_kernel, tile, inv_total), grid=(2 *...]
    psum x1 -> x0, waiting for transfers between devices: 598 us -> none  [per_device(): grad_w, a_cur, s_cur = lax.psum((w_loc, a_loc, s_loc), batch_axes)]
    unnamed x54 -> x0, local copies, waits for them, and re-layouts: 75.1 us -> none
    add x1 -> x0, other arithmetic: 37.8 us -> none  [finish(): s_new = FACTOR_DECAY * s_old + (1.0 - FACTOR_DECAY) * s_cur]
  transfers between devices with their start and end apart: 1 -> 0, of which waited for: 1 -> 0; matrix products, arithmetic and copies ran while one was open for 2% -> 0% of each run, Pallas kernels for 0% -> 0%
where the time goes in v2:
time: 821 us; the launch traced here: 820 us
  Pallas kernels  820 us (100%)
    pallas_call x1, Pallas kernels, run_stack(): pl.pallas_call(functools.partial(step_kernel, tile, inv_total), grid=(2 *...  760 us
    pallas_call x1, Pallas kernels, finish(): pl.pallas_call(finish_kernel, grid=(L,), in_specs=[pl.BlockSpec((1, DEV,...  59.9 us

profile of v2, /device:TPU:0, one launch (start us, length us, event | category | flops | bytes accessed | tf_op | source)
XLA Modules:
  0.0 820.4 jit_solution(1613757143059383350)
XLA Ops:
  0.6 759.9 %kfac_stack.1 = (bf16[7,8192,768]{2,1,0:T(8,128)(2,1)}, f32[8,8,64,768]{3,2,1,0:T(8,128)}, f32[8,8,160,768]{3,2,1,0:T(8,128)}) custom-call(bf16[8192,768]{1,0:T(8,128)(2,1)} %tok.1, bf16[8192,768]{1,0:T(8,128)(2,1)} %dout.1, bf16[8,768,768]{2,1,0:T(8,128)(2,1)} %w_ref.1, f32[8,768,768]{2,1,0:T(8,128)} %ainv.1), custom_call_target="tpu_custom_call" | custom-call | flops 318901321728 | bytes 209715200 | tf_op jit(solution)/shard_map/kfac_stack/pallas_call | solution.py:319
  760.6 59.9 %kfac_finish.1 = (f32[8,768,768]{2,1,0:T(8,128)}, f32[8,768,768]{2,1,0:T(8,128)}, f32[8,768,768]{2,1,0:T(8,128)}) custom-call(f32[8,8,64,768]{3,2,1,0:T(8,128)} %get-tuple-element.5.a_ref, f32[8,8,160,768]{3,2,1,0:T(8,128)} %get-tuple-element.6.g_ref, f32[8,768,768]{2,1,0:T(8,128)} %a_old.1, f32[8,768,768]{2,1,0:T(8,128)} %s_old.1, f32[8,768,768]{2,1,0:T(8,128)} %s_inv.1), custom_call_target="tpu_custom_call" | custom-call | flops 43486543872 | bytes 167772160 | tf_op jit(solution)/shard_map/kfac_finish/pallas_call | solution.py:383

commit v3 on v2

--- a/solution.py
+++ b/solution.py
@@ -18,7 +18,7 @@
 SR = AR + GR
 L = 8
 MESH = pl.DeviceIdType.MESH
-T1, T2, T3, T4, T5, T6, T7 = 0, 1, 5, 7, 1, 5, 7
+T1, T2, T3, T4, T5, T6, T7 = 0, 1, 4, 0, 4, 0, 2
 
 
 def tn(left, right):
@@ -75,8 +75,8 @@
 
 
 def step_kernel(tile, inv_total, tok, dout, w_ref, ainv, y_hbm, a_out, g_out,
-                buf, hbuf, ybuf, wh, acc, r1, r2a, r2b, r3a, r3b, own, ainv_v,
-                ssem, rsem, lsem, tsem, ysem, asem):
+                buf, obuf, hbuf, ybuf, wh, acc, r1, r2a, r2b, r3a, r3b, own, ainv_v,
+                ssem, rsem, lsem, tsem, ysem, osem, asem):
     w = pl.program_id(0)
     t = pl.program_id(1)
     node = lax.axis_index('node')
@@ -97,13 +97,13 @@
             pl.semaphore_signal(bar, inc=1, device_id=dev, device_id_type=MESH)
         pl.semaphore_wait(bar, 3)
         for i in range(NT):
-            pltpu.make_async_copy(tok.at[pl.ds(i * tile, tile), :], buf.at[0, i], tsem.at[i]).start()
+            pltpu.make_async_copy(tok.at[pl.ds(i * tile, tile), :], buf.at[i], tsem.at[i]).start()
 
     def rcopy(src, dst, p, k, dev):
         return pltpu.make_async_remote_copy(src_ref=src, dst_ref=dst, send_sem=ssem.at[p, k], recv_sem=rsem.at[p, k],
                                             device_id=dev, device_id_type=MESH)
 
-    def stages(rows, out, idx1, idx2, p1, p2, bwd):
+    def stages(rows, out, idx2, idx3, p1, p2, p3, bwd):
         hh = rows // 2
 
         def c1(p):
@@ -163,12 +163,12 @@
             start(c3(p1))
 
         def reduce4():
-            wait(c3(p1))
-            own[p1, 0:hh, :] = (acc[p1, me, 0:hh, :] + r3a[p1, 0:hh, :]) * inv_total
-            own[p1, hh:rows, :] = (acc[p1, me, hh:rows, :] + r3b[p1, 0:hh, :]) * inv_total
+            wait(c3(p2))
+            own[p2, 0:hh, :] = (acc[p2, me, 0:hh, :] + r3a[p2, 0:hh, :]) * inv_total
+            own[p2, hh:rows, :] = (acc[p2, me, hh:rows, :] + r3b[p2, 0:hh, :]) * inv_total
             if bwd:
-                pltpu.make_async_copy(ainv.at[L - 1 - idx1], ainv_v, asem).wait()
-                gh, gm, gl = split3(own[p1, AR:SR, :])
+                pltpu.make_async_copy(ainv.at[L - 1 - idx2], ainv_v, asem).wait()
+                gh, gm, gl = split3(own[p2, AR:SR, :])
                 g3 = jnp.concatenate([gh, gm, gl], 0)
                 g2 = jnp.concatenate([gh, gm], 0)
                 for n in range(0, D, B):
@@ -177,9 +177,9 @@
                     d2 = nt(g2, am)
                     d3 = nt(gh, al)
                     low = (d3 + d2[GR:, :]) + d1[2 * GR:, :]
-                    own[p1, AR:SR, n:n + B] = (low + (d2[0:GR, :] + d1[GR:2 * GR, :])) + d1[0:GR, :]
-            keep(p1, idx1).start()
-            start(c4(p1, idx1))
+                    own[p2, AR:SR, n:n + B] = (low + (d2[0:GR, :] + d1[GR:2 * GR, :])) + d1[0:GR, :]
+            keep(p2, idx2).start()
+            start(c4(p2, idx2))
 
         def gather5():
             keep(p2, idx2).wait()
@@ -187,38 +187,35 @@
             start(c5(p2, idx2))
 
         def gather6():
-            wait(c5(p2, idx2))
-            start(c6(p2, idx2))
+            wait(c5(p3, idx3))
+            start(c6(p3, idx3))
 
         def gather7():
-            wait(c6(p2, idx2))
+            wait(c6(p3, idx3))
 
         return reduce1, reduce2, reduce3, reduce4, gather5, gather6, gather7
 
     def at(cond, step, fn):
         pl.when(cond & (t == step))(fn)
 
-    j1, j2 = w - 1, w - 2
-    p1, p2 = lax.rem(w + 1, 2), lax.rem(w, 2)
-    fw = stages(AR, a_out, j1, j2, p1, p2, False)
-    bw = stages(SR, g_out, j1 - L, j2 - L, p1, p2, True)
-    red_f = (j1 >= 0) & (j1 < L)
-    red_b = (j1 >= L) & (j1 < 2 * L)
-    gat_f = (j2 >= 0) & (j2 < L)
-    gat_b = (j2 >= L) & (j2 < 2 * L)
-
-    @pl.when(red_b & (t == 0))
+    j1, j2, j3 = w - 1, w - 2, w - 3
+    p1, p2, p3 = lax.rem(w + 1, 2), lax.rem(w, 2), lax.rem(w + 1, 2)
+    fw = stages(AR, a_out, j2, j3, p1, p2, p3, False)
+    bw = stages(SR, g_out, j2 - L, j3 - L, p1, p2, p3, True)
+    is_f = [(j >= 0) & (j < L) for j in (j1, j2, j3)]
+    is_b = [(j >= L) & (j < 2 * L) for j in (j1, j2, j3)]
+
+    for k, (step, i) in enumerate(((T1, 0), (T2, 0), (T3, 0), (T4, 1), (T5, 1), (T6, 2), (T7, 2))):
+        at(is_f[i], step, fw[k])
+        at(is_b[i], step, bw[k])
+
+    @pl.when(is_b[0] & (t == 4))
     def _():
         pltpu.make_async_copy(ainv.at[L - 1 - (j1 - L)], ainv_v, asem).start()
-
-    for k, (step, rf, rb) in enumerate(((T1, red_f, red_b), (T2, red_f, red_b), (T3, red_f, red_b), (T4, red_f, red_b),
-                                        (T5, gat_f, gat_b), (T6, gat_f, gat_b), (T7, gat_f, gat_b))):
-        at(rf, step, fw[k])
-        at(rb, step, bw[k])
 
     p = lax.rem(w, 2)
     slot = lax.rem(t, 2)
-    half = tile // 2
+    rs = min(tile, B)
 
     @pl.when((t == 0) & (w < 2 * L))
     def _():
@@ -227,7 +224,7 @@
 
     @pl.when(w == 0)
     def _():
-        pltpu.make_async_copy(tok.at[pl.ds(t * tile, tile), :], buf.at[0, t], tsem.at[t]).wait()
+        pltpu.make_async_copy(tok.at[pl.ds(t * tile, tile), :], buf.at[t], tsem.at[t]).wait()
 
     def put_y(layer, i, s):
         return pltpu.make_async_copy(ybuf.at[s], y_hbm.at[layer, pl.ds(i * tile, tile), :], ysem.at[s])
@@ -238,28 +235,36 @@
     def get_tok(i, s):
         return pltpu.make_async_copy(tok.at[pl.ds(i * tile, tile), :], ybuf.at[s], ysem.at[s])
 
-    @pl.when((w < L) & (w * NT + t >= 2) & (w * NT + t < (L - 1) * NT + 2))
+    def put_o(i, s):
+        return pltpu.make_async_copy(obuf.at[s], buf.at[i], osem.at[s])
+
+    g_step = w * NT + t
+    fwd_out = (g_step >= 2) & (g_step < (L - 1) * NT + 2)
+
+    @pl.when(fwd_out)
     def _():
         put_y(0, 0, slot).wait()
 
+    @pl.when(fwd_out | ((g_step >= L * NT + 2) & (g_step < (2 * L - 1) * NT + 2)))
+    def _():
+        put_o(0, slot).wait()
+
     @pl.when(w < L - 1)
     def _():
-        x = buf.at[p, t]
-        for r in range(0, tile, half):
+        x = buf.at[t]
+        for r in range(0, tile, rs):
             for c in range(0, D, B):
-                y = jnp.dot(x[r:r + half, :], wh[:, c:c + B], preferred_element_type=jnp.float32).astype(jnp.bfloat16)
-                ybuf[slot, r:r + half, c:c + B] = y
-                buf[1 - p, t, r:r + half, c:c + B] = gelu_value(y)
+                y = jnp.dot(x[r:r + rs, :], wh[:, c:c + B], preferred_element_type=jnp.float32).astype(jnp.bfloat16)
+                ybuf[slot, r:r + rs, c:c + B] = y
+                obuf[slot, r:r + rs, c:c + B] = gelu_value(y)
         gram_add(acc, p, x[...])
         put_y(w, t, slot).start()
+        put_o(t, slot).start()
 
     @pl.when(w == L - 1)
     def _():
-        @pl.when(t == 0)
-        def _():
-            for i in range(NT):
-                pltpu.make_async_copy(dout.at[pl.ds(i * tile, tile), :], buf.at[0, i], tsem.at[i]).start()
-        gram_add(acc, p, buf[p, t])
+        gram_add(acc, p, buf[t])
+        pltpu.make_async_copy(dout.at[pl.ds(t * tile, tile), :], buf.at[t], tsem.at[t]).start()
 
         @pl.when(t == NT - 1)
         def _():
@@ -267,7 +272,7 @@
 
     @pl.when(w == L)
     def _():
-        pltpu.make_async_copy(dout.at[pl.ds(t * tile, tile), :], buf.at[0, t], tsem.at[t]).wait()
+        pltpu.make_async_copy(dout.at[pl.ds(t * tile, tile), :], buf.at[t], tsem.at[t]).wait()
 
     wn = jnp.where(t == NT - 1, w + 1, w)
     tn_ = jnp.where(t == NT - 1, 0, t + 1)
@@ -290,19 +295,20 @@
 
     @pl.when((w >= L) & (w < 2 * L - 1))
     def _():
-        g = buf.at[p, t]
-        for r in range(0, tile, half):
+        g = buf.at[t]
+        for r in range(0, tile, rs):
             for c in range(0, D, B):
-                dh = nt(g[r:r + half, :], wh[c:c + B, :]).astype(jnp.bfloat16)
-                h, slope2 = gelu_both(ybuf[slot, r:r + half, c:c + B])
-                hbuf[r:r + half, c:c + B] = h
-                buf[1 - p, t, r:r + half, c:c + B] = (dh.astype(jnp.float32) * slope2).astype(jnp.bfloat16)
+                dh = nt(g[r:r + rs, :], wh[c:c + B, :]).astype(jnp.bfloat16)
+                h, slope2 = gelu_both(ybuf[slot, r:r + rs, c:c + B])
+                hbuf[r:r + rs, c:c + B] = h
+                obuf[slot, r:r + rs, c:c + B] = (dh.astype(jnp.float32) * slope2).astype(jnp.bfloat16)
         gram_add(acc, p, g[...])
         grad_add(g[...], hbuf[...])
+        put_o(t, slot).start()
 
     @pl.when(w == 2 * L - 1)
     def _():
-        g = buf[p, t]
+        g = buf[t]
         gram_add(acc, p, g)
         grad_add(g, ybuf[slot])
 
@@ -318,7 +324,7 @@
 
     return pl.pallas_call(
         functools.partial(step_kernel, tile, inv_total),
-        grid=(2 * L + 2, NT),
+        grid=(2 * L + 3, NT),
         in_specs=[any_spec, any_spec, pl.BlockSpec((1, d, d), w_map), any_spec],
         out_specs=[any_spec] * 3,
         out_shape=[
@@ -327,7 +333,8 @@
             jax.ShapeDtypeStruct((L, DEV, SR, d), f32),
         ],
         scratch_shapes=[
-            pltpu.VMEM((2, NT, tile, d), bf16),
+            pltpu.VMEM((NT, tile, d), bf16),
+            pltpu.VMEM((2, tile, d), bf16),
             pltpu.VMEM((tile, d), bf16),
             pltpu.VMEM((2, tile, d), bf16),
             pltpu.VMEM((d, d), bf16),
@@ -343,6 +350,7 @@
             pltpu.SemaphoreType.DMA((2, 20)),
             pltpu.SemaphoreType.DMA((2,)),
             pltpu.SemaphoreType.DMA((NT,)),
+            pltpu.SemaphoreType.DMA((2,)),
             pltpu.SemaphoreType.DMA((2,)),
             pltpu.SemaphoreType.DMA,
         ],

time: 821 us -> 591 us (0.72)
  Pallas kernels: 820 us -> 590 us
    pallas_call x1, Pallas kernels: 760 us -> 530 us  [run_stack(): pl.pallas_call(functools.partial(step_kernel, tile, inv_total), grid=(2 *...]
where the time goes in v3:
time: 591 us
  Pallas kernels  590 us (100%)
    pallas_call x1, Pallas kernels, run_stack(): pl.pallas_call(functools.partial(step_kernel, tile, inv_total), grid=(2 *...  530 us
    pallas_call x1, Pallas kernels, finish(): pl.pallas_call(finish_kernel, grid=(L,), in_specs=[pl.BlockSpec((1, DEV,...  60 us

profile of v3, /device:TPU:0, one launch (start us, length us, event | category | flops | bytes accessed | tf_op | source)
XLA Modules:
  0.0 590.9 jit_solution(9957296097520274440)
XLA Ops:
  0.6 530.3 %kfac_stack.1 = (bf16[7,8192,768]{2,1,0:T(8,128)(2,1)}, f32[8,8,64,768]{3,2,1,0:T(8,128)}, f32[8,8,160,768]{3,2,1,0:T(8,128)}) custom-call(bf16[8192,768]{1,0:T(8,128)(2,1)} %tok.1, bf16[8192,768]{1,0:T(8,128)(2,1)} %dout.1, bf16[8,768,768]{2,1,0:T(8,128)(2,1)} %w_ref.1, f32[8,768,768]{2,1,0:T(8,128)} %ainv.1), custom_call_target="tpu_custom_call" | custom-call | flops 318901321728 | bytes 209715200 | tf_op jit(solution)/shard_map/kfac_stack/pallas_call | solution.py:325
  530.9 60.0 %kfac_finish.1 = (f32[8,768,768]{2,1,0:T(8,128)}, f32[8,768,768]{2,1,0:T(8,128)}, f32[8,768,768]{2,1,0:T(8,128)}) custom-call(f32[8,8,64,768]{3,2,1,0:T(8,128)} %get-tuple-element.5.a_ref, f32[8,8,160,768]{3,2,1,0:T(8,128)} %get-tuple-element.6.g_ref, f32[8,768,768]{2,1,0:T(8,128)} %a_old.1, f32[8,768,768]{2,1,0:T(8,128)} %s_old.1, f32[8,768,768]{2,1,0:T(8,128)} %s_inv.1), custom_call_target="tpu_custom_call" | custom-call | flops 43486543872 | bytes 167772160 | tf_op jit(solution)/shard_map/kfac_finish/pallas_call | solution.py:391

commit v4 on v3

--- a/solution.py
+++ b/solution.py
@@ -18,7 +18,7 @@
 SR = AR + GR
 L = 8
 MESH = pl.DeviceIdType.MESH
-T1, T2, T3, T4, T5, T6, T7 = 0, 1, 4, 0, 4, 0, 2
+T1, T2, T3, T4, T5, T6, T7 = 0, 1, 0, 4, 2, 2, 4
 
 
 def tn(left, right):
@@ -103,21 +103,21 @@
         return pltpu.make_async_remote_copy(src_ref=src, dst_ref=dst, send_sem=ssem.at[p, k], recv_sem=rsem.at[p, k],
                                             device_id=dev, device_id_type=MESH)
 
-    def stages(rows, out, idx2, idx3, p1, p2, p3, bwd):
+    def stages(rows, out, idx2, idx3, idx4, bwd):
         hh = rows // 2
 
-        def c1(p):
-            return [rcopy(acc.at[p, chunk(i // 2, i % 2, 1 - cc), pl.ds(0, rows)], r1.at[p, i, pl.ds(0, rows)], p, i, partner)
+        def c1(p, q):
+            return [rcopy(acc.at[q, chunk(i // 2, i % 2, 1 - cc), pl.ds(0, rows)], r1.at[p, i, pl.ds(0, rows)], p, i, partner)
                     for i in range(4)]
 
-        def c2(p):
-            a = [rcopy(acc.at[p, chunk(i, 1 - cx, cc), pl.ds(0, hh)], r2a.at[p, i, pl.ds(0, hh)], p, 4 + i, xn) for i in range(2)]
-            b = [rcopy(acc.at[p, chunk(1 - cy, i, cc), pl.ds(hh, hh)], r2b.at[p, i, pl.ds(0, hh)], p, 6 + i, yn) for i in range(2)]
+        def c2(p, q):
+            a = [rcopy(acc.at[q, chunk(i, 1 - cx, cc), pl.ds(0, hh)], r2a.at[p, i, pl.ds(0, hh)], p, 4 + i, xn) for i in range(2)]
+            b = [rcopy(acc.at[q, chunk(1 - cy, i, cc), pl.ds(hh, hh)], r2b.at[p, i, pl.ds(0, hh)], p, 6 + i, yn) for i in range(2)]
             return a + b
 
-        def c3(p):
-            return [rcopy(acc.at[p, chunk(1 - cy, cx, cc), pl.ds(0, hh)], r3a.at[p, pl.ds(0, hh)], p, 8, yn),
-                    rcopy(acc.at[p, chunk(cy, 1 - cx, cc), pl.ds(hh, hh)], r3b.at[p, pl.ds(0, hh)], p, 9, xn)]
+        def c3(p, q):
+            return [rcopy(acc.at[q, chunk(1 - cy, cx, cc), pl.ds(0, hh)], r3a.at[p, pl.ds(0, hh)], p, 8, yn),
+                    rcopy(acc.at[q, chunk(cy, 1 - cx, cc), pl.ds(hh, hh)], r3b.at[p, pl.ds(0, hh)], p, 9, xn)]
 
         def c4(p, idx):
             return [rcopy(own.at[p, pl.ds(0, hh)], out.at[idx, me, pl.ds(0, hh)], p, 10, yn),
@@ -147,25 +147,25 @@
                 c.wait()
 
         def reduce1():
-            start(c1(p1))
+            start(c1(p1, q1))
 
         def reduce2():
-            wait(c1(p1))
+            wait(c1(p1, q1))
             for i in range(4):
-                acc[p1, chunk(i // 2, i % 2, cc), 0:rows, :] += r1[p1, i, 0:rows, :]
-            start(c2(p1))
+                acc[q1, chunk(i // 2, i % 2, cc), 0:rows, :] += r1[p1, i, 0:rows, :]
+            start(c2(p1, q1))
 
         def reduce3():
-            wait(c2(p1))
+            wait(c2(p2, q2))
             for i in range(2):
-                acc[p1, chunk(i, cx, cc), 0:hh, :] += r2a[p1, i, 0:hh, :]
-                acc[p1, chunk(cy, i, cc), hh:rows, :] += r2b[p1, i, 0:hh, :]
-            start(c3(p1))
+                acc[q2, chunk(i, cx, cc), 0:hh, :] += r2a[p2, i, 0:hh, :]
+                acc[q2, chunk(cy, i, cc), hh:rows, :] += r2b[p2, i, 0:hh, :]
+            start(c3(p2, q2))
 
         def reduce4():
-            wait(c3(p2))
-            own[p2, 0:hh, :] = (acc[p2, me, 0:hh, :] + r3a[p2, 0:hh, :]) * inv_total
-            own[p2, hh:rows, :] = (acc[p2, me, hh:rows, :] + r3b[p2, 0:hh, :]) * inv_total
+            wait(c3(p2, q2))
+            own[p2, 0:hh, :] = (acc[q2, me, 0:hh, :] + r3a[p2, 0:hh, :]) * inv_total
+            own[p2, hh:rows, :] = (acc[q2, me, hh:rows, :] + r3b[p2, 0:hh, :]) * inv_total
             if bwd:
                 pltpu.make_async_copy(ainv.at[L - 1 - idx2], ainv_v, asem).wait()
                 gh, gm, gl = split3(own[p2, AR:SR, :])
@@ -182,38 +182,39 @@
             start(c4(p2, idx2))
 
         def gather5():
-            keep(p2, idx2).wait()
-            wait(c4(p2, idx2))
-            start(c5(p2, idx2))
+            keep(p3, idx3).wait()
+            wait(c4(p3, idx3))
+            start(c5(p3, idx3))
 
         def gather6():
-            wait(c5(p3, idx3))
-            start(c6(p3, idx3))
+            wait(c5(p4, idx4))
+            start(c6(p4, idx4))
 
         def gather7():
-            wait(c6(p3, idx3))
+            wait(c6(p4, idx4))
 
         return reduce1, reduce2, reduce3, reduce4, gather5, gather6, gather7
 
     def at(cond, step, fn):
         pl.when(cond & (t == step))(fn)
 
-    j1, j2, j3 = w - 1, w - 2, w - 3
-    p1, p2, p3 = lax.rem(w + 1, 2), lax.rem(w, 2), lax.rem(w + 1, 2)
-    fw = stages(AR, a_out, j2, j3, p1, p2, p3, False)
-    bw = stages(SR, g_out, j2 - L, j3 - L, p1, p2, p3, True)
-    is_f = [(j >= 0) & (j < L) for j in (j1, j2, j3)]
-    is_b = [(j >= L) & (j < 2 * L) for j in (j1, j2, j3)]
-
-    for k, (step, i) in enumerate(((T1, 0), (T2, 0), (T3, 0), (T4, 1), (T5, 1), (T6, 2), (T7, 2))):
+    j1, j2, j3, j4 = w - 1, w - 2, w - 3, w - 4
+    p1, p2, p3, p4 = lax.rem(w + 1, 2), lax.rem(w, 2), lax.rem(w + 1, 2), lax.rem(w, 2)
+    q1, q2 = lax.rem(w + 2, 3), lax.rem(w + 1, 3)
+    fw = stages(AR, a_out, j2, j3, j4, False)
+    bw = stages(SR, g_out, j2 - L, j3 - L, j4 - L, True)
+    is_f = [(j >= 0) & (j < L) for j in (j1, j2, j3, j4)]
+    is_b = [(j >= L) & (j < 2 * L) for j in (j1, j2, j3, j4)]
+
+    @pl.when(is_b[1] & (t == 0))
+    def _():
+        pltpu.make_async_copy(ainv.at[L - 1 - (j2 - L)], ainv_v, asem).start()
+
+    for k, step, i in ((0, T1, 0), (2, T3, 1), (1, T2, 0), (5, T6, 3), (4, T5, 2), (3, T4, 1), (6, T7, 3)):
         at(is_f[i], step, fw[k])
         at(is_b[i], step, bw[k])
 
-    @pl.when(is_b[0] & (t == 4))
-    def _():
-        pltpu.make_async_copy(ainv.at[L - 1 - (j1 - L)], ainv_v, asem).start()
-
-    p = lax.rem(w, 2)
+    p = lax.rem(w, 3)
     slot = lax.rem(t, 2)
     rs = min(tile, B)
 
@@ -324,7 +325,7 @@
 
     return pl.pallas_call(
         functools.partial(step_kernel, tile, inv_total),
-        grid=(2 * L + 3, NT),
+        grid=(2 * L + 4, NT),
         in_specs=[any_spec, any_spec, pl.BlockSpec((1, d, d), w_map), any_spec],
         out_specs=[any_spec] * 3,
         out_shape=[
@@ -338,7 +339,7 @@
             pltpu.VMEM((tile, d), bf16),
             pltpu.VMEM((2, tile, d), bf16),
             pltpu.VMEM((d, d), bf16),
-            pltpu.VMEM((2, DEV, SR, d), f32),
+            pltpu.VMEM((3, DEV, SR, d), f32),
             pltpu.VMEM((2, 4, SR, d), f32),
             pltpu.VMEM((2, 2, SR // 2, d), f32),
             pltpu.VMEM((2, 2, SR // 2, d), f32),

time: 591 us -> 601 us (1.017)
  Pallas kernels: 590 us -> 600 us
    pallas_call x1, Pallas kernels: 530 us -> 540 us  [run_stack(): pl.pallas_call(functools.partial(step_kernel, tile, inv_total), grid=(2 *...]
where the time goes in v4:
time: 601 us; the launch traced here: 600 us
  Pallas kernels  600 us (100%)
    pallas_call x1, Pallas kernels, run_stack(): pl.pallas_call(functools.partial(step_kernel, tile, inv_total), grid=(2 *...  540 us
    pallas_call x1, Pallas kernels, finish(): pl.pallas_call(finish_kernel, grid=(L,), in_specs=[pl.BlockSpec((1, DEV,...  60 us

profile of v4, /device:TPU:0, one launch (start us, length us, event | category | flops | bytes accessed | tf_op | source)
XLA Modules:
  0.0 600.4 jit_solution(10189708884079823286)
XLA Ops:
  0.6 539.8 %kfac_stack.1 = (bf16[7,8192,768]{2,1,0:T(8,128)(2,1)}, f32[8,8,64,768]{3,2,1,0:T(8,128)}, f32[8,8,160,768]{3,2,1,0:T(8,128)}) custom-call(bf16[8192,768]{1,0:T(8,128)(2,1)} %tok.1, bf16[8192,768]{1,0:T(8,128)(2,1)} %dout.1, bf16[8,768,768]{2,1,0:T(8,128)(2,1)} %w_ref.1, f32[8,768,768]{2,1,0:T(8,128)} %ainv.1), custom_call_target="tpu_custom_call" | custom-call | flops 318901321728 | bytes 209715200 | tf_op jit(solution)/shard_map/kfac_stack/pallas_call | solution.py:326
  540.4 60.0 %kfac_finish.1 = (f32[8,768,768]{2,1,0:T(8,128)}, f32[8,768,768]{2,1,0:T(8,128)}, f32[8,768,768]{2,1,0:T(8,128)}) custom-call(f32[8,8,64,768]{3,2,1,0:T(8,128)} %get-tuple-element.5.a_ref, f32[8,8,160,768]{3,2,1,0:T(8,128)} %get-tuple-element.6.g_ref, f32[8,768,768]{2,1,0:T(8,128)} %a_old.1, f32[8,768,768]{2,1,0:T(8,128)} %s_old.1, f32[8,768,768]{2,1,0:T(8,128)} %s_inv.1), custom_call_target="tpu_custom_call" | custom-call | flops 43486543872 | bytes 167772160 | tf_op jit(solution)/shard_map/kfac_finish/pallas_call | solution.py:392

commit v5 on v4

--- a/solution.py
+++ b/solution.py
@@ -11,9 +11,10 @@
 GELU_CUBIC = 0.044715
 D = 768
 B = 256
+H = 128
 NT = 8
 DEV = 8
-AR = 64
+AR = 48
 GR = 96
 SR = AR + GR
 L = 8
@@ -60,10 +61,42 @@
         r += k
 
 
-def gram_add(acc, p, x):
-    add_rows(acc, p, 0, AR, 0, 0, tn(x[:, 0:B], x))
-    add_rows(acc, p, 0, AR, B, 0, tn(x[:, B:2 * B], x[:, B:]))
-    add_rows(acc, p, 0, AR, B, 2 * B, tn(x[:, 2 * B:], x[:, 2 * B:]))
+def set_rows(acc, q, first, c0, val):
+    r = first
+    while r < first + val.shape[0]:
+        d, o = divmod(r, AR)
+        k = min(AR - o, first + val.shape[0] - r)
+        acc[q, d, o:o + k, c0:c0 + val.shape[1]] = val[r - first:r - first + k, :]
+        r += k
+
+
+def gram_add(acc, dg, p, x):
+    top = tn(x[:, 0:B], x)
+    dg[0] += top[:, 0:B]
+    add_rows(acc, p, 0, AR, 0, B, top[:, B:])
+    mid = tn(x[:, B:2 * B], x[:, B:])
+    dg[1] += mid[:, 0:B]
+    add_rows(acc, p, 0, AR, B, 0, mid[0:H, B:])
+    add_rows(acc, p, 0, AR, B, B, mid[H:, B:])
+    dg[2] += tn(x[:, 2 * B:], x[:, 2 * B:])
+
+
+def row_col(n):
+    return lax.broadcasted_iota(jnp.int32, (n, n), 0), lax.broadcasted_iota(jnp.int32, (n, n), 1)
+
+
+def pack_diag(acc, ex, dg, q):
+    r, c = row_col(B)
+    rh, ch = row_col(H)
+    d0, d1, d2 = dg[0], dg[1], dg[2]
+    set_rows(acc, q, 0, 0, jnp.where(c >= r, d0, d1))
+    set_rows(acc, q, B, 2 * B, jnp.where(ch >= rh, d2[0:H, 0:H], d2[H:, H:]))
+    set_rows(acc, q, B, 2 * B + H, d2[0:H, H:])
+    v1 = jnp.sum(jnp.where(c == r, d1, 0.0), axis=0, keepdims=True)
+    v2 = jnp.sum(jnp.where(ch == rh, d2[H:, H:], 0.0), axis=0, keepdims=True)
+    ex[q, :, 0:B] = jnp.broadcast_to(v1, (8, B))
+    ex[q, :, B:B + H] = jnp.broadcast_to(v2, (8, H))
+    ex[q, :, B + H:] = jnp.zeros((8, D - B - H), jnp.float32)
 
 
 def split3(x):
@@ -74,9 +107,9 @@
     return hi, mid, lo
 
 
-def step_kernel(tile, inv_total, tok, dout, w_ref, ainv, y_hbm, a_out, g_out,
-                buf, obuf, hbuf, ybuf, wh, acc, r1, r2a, r2b, r3a, r3b, own, ainv_v,
-                ssem, rsem, lsem, tsem, ysem, osem, asem):
+def step_kernel(tile, inv_total, tok, dout, w_ref, ainv, y_hbm, a_out, g_out, ax_out, gx_out,
+                buf, obuf, hbuf, ybuf, wh, acc, dg, ex, exr, r1, r2a, r2b, r3a, r3b, own, ainv_v,
+                ssem, rsem, lsem, xsem, tsem, ysem, osem, asem):
     w = pl.program_id(0)
     t = pl.program_id(1)
     node = lax.axis_index('node')
@@ -103,21 +136,22 @@
         return pltpu.make_async_remote_copy(src_ref=src, dst_ref=dst, send_sem=ssem.at[p, k], recv_sem=rsem.at[p, k],
                                             device_id=dev, device_id_type=MESH)
 
-    def stages(rows, out, idx2, idx3, idx4, bwd):
+    def stages(rows, out, xout, idx2, idx3, idx4, bwd):
         hh = rows // 2
 
         def c1(p, q):
             return [rcopy(acc.at[q, chunk(i // 2, i % 2, 1 - cc), pl.ds(0, rows)], r1.at[p, i, pl.ds(0, rows)], p, i, partner)
-                    for i in range(4)]
+                    for i in range(4)] + [rcopy(ex.at[q], exr.at[p, 0], p, 20, partner)]
 
         def c2(p, q):
             a = [rcopy(acc.at[q, chunk(i, 1 - cx, cc), pl.ds(0, hh)], r2a.at[p, i, pl.ds(0, hh)], p, 4 + i, xn) for i in range(2)]
             b = [rcopy(acc.at[q, chunk(1 - cy, i, cc), pl.ds(hh, hh)], r2b.at[p, i, pl.ds(0, hh)], p, 6 + i, yn) for i in range(2)]
-            return a + b
+            return a + b + [rcopy(ex.at[q], exr.at[p, 1], p, 21, xn)]
 
         def c3(p, q):
             return [rcopy(acc.at[q, chunk(1 - cy, cx, cc), pl.ds(0, hh)], r3a.at[p, pl.ds(0, hh)], p, 8, yn),
-                    rcopy(acc.at[q, chunk(cy, 1 - cx, cc), pl.ds(hh, hh)], r3b.at[p, pl.ds(0, hh)], p, 9, xn)]
+                    rcopy(acc.at[q, chunk(cy, 1 - cx, cc), pl.ds(hh, hh)], r3b.at[p, pl.ds(0, hh)], p, 9, xn),
+                    rcopy(ex.at[q], exr.at[p, 2], p, 22, yn)]
 
         def c4(p, idx):
             return [rcopy(own.at[p, pl.ds(0, hh)], out.at[idx, me, pl.ds(0, hh)], p, 10, yn),
@@ -125,6 +159,9 @@
 
         def keep(p, idx):
             return pltpu.make_async_copy(own.at[p, pl.ds(0, rows)], out.at[idx, me], lsem.at[p])
+
+        def keep_x(p, q, idx):
+            return pltpu.make_async_copy(ex.at[q], xout.at[idx], xsem.at[p])
 
         def c5(p, idx):
             def mv(d, o, k, dev):
@@ -147,16 +184,19 @@
                 c.wait()
 
         def reduce1():
+            pack_diag(acc, ex, dg, q1)
             start(c1(p1, q1))
 
         def reduce2():
             wait(c1(p1, q1))
+            ex[q1] += exr[p1, 0]
             for i in range(4):
                 acc[q1, chunk(i // 2, i % 2, cc), 0:rows, :] += r1[p1, i, 0:rows, :]
             start(c2(p1, q1))
 
         def reduce3():
             wait(c2(p2, q2))
+            ex[q2] += exr[p2, 1]
             for i in range(2):
                 acc[q2, chunk(i, cx, cc), 0:hh, :] += r2a[p2, i, 0:hh, :]
                 acc[q2, chunk(cy, i, cc), hh:rows, :] += r2b[p2, i, 0:hh, :]
@@ -164,6 +204,7 @@
 
         def reduce4():
             wait(c3(p2, q2))
+            ex[q2] = (ex[q2] + exr[p2, 2]) * inv_total
             own[p2, 0:hh, :] = (acc[q2, me, 0:hh, :] + r3a[p2, 0:hh, :]) * inv_total
             own[p2, hh:rows, :] = (acc[q2, me, hh:rows, :] + r3b[p2, 0:hh, :]) * inv_total
             if bwd:
@@ -179,10 +220,12 @@
                     low = (d3 + d2[GR:, :]) + d1[2 * GR:, :]
                     own[p2, AR:SR, n:n + B] = (low + (d2[0:GR, :] + d1[GR:2 * GR, :])) + d1[0:GR, :]
             keep(p2, idx2).start()
+            keep_x(p2, q2, idx2).start()
             start(c4(p2, idx2))
 
         def gather5():
             keep(p3, idx3).wait()
+            keep_x(p3, q3, idx3).wait()
             wait(c4(p3, idx3))
             start(c5(p3, idx3))
 
@@ -200,9 +243,9 @@
 
     j1, j2, j3, j4 = w - 1, w - 2, w - 3, w - 4
     p1, p2, p3, p4 = lax.rem(w + 1, 2), lax.rem(w, 2), lax.rem(w + 1, 2), lax.rem(w, 2)
-    q1, q2 = lax.rem(w + 2, 3), lax.rem(w + 1, 3)
-    fw = stages(AR, a_out, j2, j3, j4, False)
-    bw = stages(SR, g_out, j2 - L, j3 - L, j4 - L, True)
+    q1, q2, q3 = lax.rem(w + 2, 3), lax.rem(w + 1, 3), lax.rem(w, 3)
+    fw = stages(AR, a_out, ax_out, j2, j3, j4, False)
+    bw = stages(SR, g_out, gx_out, j2 - L, j3 - L, j4 - L, True)
     is_f = [(j >= 0) & (j < L) for j in (j1, j2, j3, j4)]
     is_b = [(j >= L) & (j < 2 * L) for j in (j1, j2, j3, j4)]
 
@@ -221,6 +264,7 @@
     @pl.when((t == 0) & (w < 2 * L))
     def _():
         acc[p] = jnp.zeros(acc.shape[1:], jnp.float32)
+        dg[...] = jnp.zeros_like(dg)
         wh[...] = w_ref[0] * jnp.bfloat16(0.5)
 
     @pl.when(w == 0)
@@ -258,13 +302,13 @@
                 y = jnp.dot(x[r:r + rs, :], wh[:, c:c + B], preferred_element_type=jnp.float32).astype(jnp.bfloat16)
                 ybuf[slot, r:r + rs, c:c + B] = y
                 obuf[slot, r:r + rs, c:c + B] = gelu_value(y)
-        gram_add(acc, p, x[...])
+        gram_add(acc, dg, p, x[...])
         put_y(w, t, slot).start()
         put_o(t, slot).start()
 
     @pl.when(w == L - 1)
     def _():
-        gram_add(acc, p, buf[t])
+        gram_add(acc, dg, p, buf[t])
         pltpu.make_async_copy(dout.at[pl.ds(t * tile, tile), :], buf.at[t], tsem.at[t]).start()
 
         @pl.when(t == NT - 1)
@@ -303,14 +347,14 @@
                 h, slope2 = gelu_both(ybuf[slot, r:r + rs, c:c + B])
                 hbuf[r:r + rs, c:c + B] = h
                 obuf[slot, r:r + rs, c:c + B] = (dh.astype(jnp.float32) * slope2).astype(jnp.bfloat16)
-        gram_add(acc, p, g[...])
+        gram_add(acc, dg, p, g[...])
         grad_add(g[...], hbuf[...])
         put_o(t, slot).start()
 
     @pl.when(w == 2 * L - 1)
     def _():
         g = buf[t]
-        gram_add(acc, p, g)
+        gram_add(acc, dg, p, g)
         grad_add(g, ybuf[slot])
 
 
@@ -327,11 +371,13 @@
         functools.partial(step_kernel, tile, inv_total),
         grid=(2 * L + 4, NT),
         in_specs=[any_spec, any_spec, pl.BlockSpec((1, d, d), w_map), any_spec],
-        out_specs=[any_spec] * 3,
+        out_specs=[any_spec] * 5,
         out_shape=[
             jax.ShapeDtypeStruct((L - 1, n, d), bf16),
             jax.ShapeDtypeStruct((L, DEV, AR, d), f32),
             jax.ShapeDtypeStruct((L, DEV, SR, d), f32),
+            jax.ShapeDtypeStruct((L, 8, d), f32),
+            jax.ShapeDtypeStruct((L, 8, d), f32),
         ],
         scratch_shapes=[
             pltpu.VMEM((NT, tile, d), bf16),
@@ -340,6 +386,9 @@
             pltpu.VMEM((2, tile, d), bf16),
             pltpu.VMEM((d, d), bf16),
             pltpu.VMEM((3, DEV, SR, d), f32),
+            pltpu.VMEM((3, B, B), f32),
+            pltpu.VMEM((3, 8, d), f32),
+            pltpu.VMEM((2, 3, 8, d), f32),
             pltpu.VMEM((2, 4, SR, d), f32),
             pltpu.VMEM((2, 2, SR // 2, d), f32),
             pltpu.VMEM((2, 2, SR // 2, d), f32),
@@ -347,8 +396,9 @@
             pltpu.VMEM((2, SR // 2, d), f32),
             pltpu.VMEM((2, SR, d), f32),
             pltpu.VMEM((d, d), f32),
-            pltpu.SemaphoreType.DMA((2, 20)),
-            pltpu.SemaphoreType.DMA((2, 20)),
+            pltpu.SemaphoreType.DMA((2, 23)),
+            pltpu.SemaphoreType.DMA((2, 23)),
+            pltpu.SemaphoreType.DMA((2,)),
             pltpu.SemaphoreType.DMA((2,)),
             pltpu.SemaphoreType.DMA((NT,)),
             pltpu.SemaphoreType.DMA((2,)),
@@ -361,21 +411,46 @@
     )(tok, dout, w, a_inv)
 
 
-def finish_kernel(a_ref, g_ref, a_old, s_old, s_inv, upd, a_new, s_new):
-    def unfold(p, old, new):
-        sc = (1.0 - FACTOR_DECAY)
-
-        def put(r, c, val):
-            new[0, r * B:(r + 1) * B, c * B:(c + 1) * B] = FACTOR_DECAY * old[0, r * B:(r + 1) * B, c * B:(c + 1) * B] + sc * val
-
-        for (pr, pc, r, c) in ((0, 0, 0, 0), (0, 1, 0, 1), (0, 2, 0, 2), (1, 0, 1, 1), (1, 1, 1, 2), (1, 2, 2, 2)):
-            blk = jnp.concatenate([p[0, d, 0:AR, pc * B:(pc + 1) * B] for d in range(pr * 4, pr * 4 + 4)], 0)
-            put(r, c, blk)
-            if r != c:
-                put(c, r, blk.T)
-
-    unfold(a_ref, a_old, a_new)
-    unfold(g_ref, s_old, s_new)
+def finish_kernel(a_ref, g_ref, ax_ref, gx_ref, a_old, s_old, s_inv, upd, a_new, s_new):
+    r, c = row_col(B)
+    rh, ch = row_col(H)
+
+    def unfold(p, x, old, new):
+        def put(r0, c0, val):
+            rs, cs = slice(r0, r0 + val.shape[0]), slice(c0, c0 + val.shape[1])
+            new[0, rs, cs] = FACTOR_DECAY * old[0, rs, cs] + (1.0 - FACTOR_DECAY) * val
+
+        def rows(first, n, c0, width):
+            parts, k = [], first
+            while k < first + n:
+                d, o = divmod(k, AR)
+                m = min(AR - o, first + n - k)
+                parts.append(p[0, d, o:o + m, c0:c0 + width])
+                k += m
+            return jnp.concatenate(parts, 0)
+
+        both = rows(0, B, 0, B)
+        flip = both.T
+        put(0, 0, jnp.where(c >= r, both, flip))
+        put(B, B, jnp.where(c == r, x[0, 0:1, 0:B], jnp.where(c < r, both, flip)))
+        for c0 in (B, 2 * B):
+            blk = rows(0, B, c0, B)
+            put(0, c0, blk)
+            put(c0, 0, blk.T)
+        for i in range(2):
+            blk = rows(B, H, i * B, B)
+            put(B + i * H, 2 * B, blk)
+            put(2 * B, B + i * H, blk.T)
+        both = rows(B, H, 2 * B, H)
+        flip = both.T
+        put(2 * B, 2 * B, jnp.where(ch >= rh, both, flip))
+        put(2 * B + H, 2 * B + H, jnp.where(ch == rh, x[0, 0:1, B:B + H], jnp.where(ch < rh, both, flip)))
+        blk = rows(B, H, 2 * B + H, H)
+        put(2 * B, 2 * B + H, blk)
+        put(2 * B + H, 2 * B, blk.T)
+
+    unfold(a_ref, ax_ref, a_old, a_new)
+    unfold(g_ref, gx_ref, s_old, s_new)
     sh, sm, sl = split3(s_inv[0])
     lt = jnp.concatenate([g_ref[0, d, AR:SR, :] for d in range(DEV)], 0)
     lh, lm, ll = split3(lt)
@@ -385,7 +460,7 @@
         upd[0, m:m + B, :] = (low + (tn(x, sm) + tn(y, sh))) + tn(x, sh)
 
 
-def finish(a_red, g_red, a_old, s_old, s_inv):
+def finish(a_red, g_red, a_ex, g_ex, a_old, s_old, s_inv):
     f32 = jnp.float32
     full = pl.BlockSpec((1, D, D), lambda l: (l, 0, 0))
     shape = jax.ShapeDtypeStruct((L, D, D), f32)
@@ -395,6 +470,8 @@
         in_specs=[
             pl.BlockSpec((1, DEV, AR, D), lambda l: (l, 0, 0, 0)),
             pl.BlockSpec((1, DEV, SR, D), lambda l: (L - 1 - l, 0, 0, 0)),
+            pl.BlockSpec((1, 8, D), lambda l: (l, 0, 0)),
+            pl.BlockSpec((1, 8, D), lambda l: (L - 1 - l, 0, 0)),
             full, full, full,
         ],
         out_specs=[full] * 3,
@@ -402,7 +479,7 @@
         compiler_params=pltpu.CompilerParams(vmem_limit_bytes=60 * 2 ** 20),
         cost_estimate=pl.CostEstimate(flops=L * 12 * D ** 3, bytes_accessed=160 * 2 ** 20, transcendentals=0),
         name="kfac_finish",
-    )(a_red, g_red, a_old, s_old, s_inv)
+    )(a_red, g_red, a_ex, g_ex, a_old, s_old, s_inv)
 
 
 def solution(mesh):
@@ -414,8 +491,8 @@
         inv_total = 1.0 / tokens.shape[0]
 
         def per_device(tok, dout, w, a_prev, s_prev, a_pre, s_pre):
-            _, a_red, g_red = run_stack(tok, dout, w, a_pre, inv_total)
-            return tuple(finish(a_red, g_red, a_prev, s_prev, s_pre))
+            _, a_red, g_red, a_ex, g_ex = run_stack(tok, dout, w, a_pre, inv_total)
+            return tuple(finish(a_red, g_red, a_ex, g_ex, a_prev, s_prev, s_pre))
 
         return jax.shard_map(per_device, mesh=mesh, in_specs=(row_spec, row_spec, full_spec, full_spec, full_spec, full_spec, full_spec), out_specs=(full_spec, full_spec, full_spec), check_vma=False)(tokens, grad_out, weights, a_old, s_old, a_inv, s_inv)
 

time: 601 us -> 590 us (0.982)
  Pallas kernels: 600 us -> 589 us
    pallas_call x1, Pallas kernels: 540 us -> 532 us  [run_stack(): pl.pallas_call(functools.partial(step_kernel, tile, inv_total), grid=(2 *...]
where the time goes in v5:
time: 590 us
  Pallas kernels  589 us (100%)
    pallas_call x1, Pallas kernels, run_stack(): pl.pallas_call(functools.partial(step_kernel, tile, inv_total), grid=(2 *...  532 us
    pallas_call x1, Pallas kernels, finish(): pl.pallas_call(finish_kernel, grid=(L,), in_specs=[pl.BlockSpec((1, DEV,...  57.4 us

profile of v5, /device:TPU:0, one launch (start us, length us, event | category | flops | bytes accessed | tf_op | source)
XLA Modules:
  0.0 590.0 jit_solution(14596356597397723641)
XLA Ops:
  0.6 532.0 %kfac_stack.1 = (bf16[7,8192,768]{2,1,0:T(8,128)(2,1)}, f32[8,8,48,768]{3,2,1,0:T(8,128)}, f32[8,8,144,768]{3,2,1,0:T(8,128)}, f32[8,8,768]{2,1,0:T(8,128)}, f32[8,8,768]{2,1,0:T(8,128)}) custom-call(bf16[8192,768]{1,0:T(8,128)(2,1)} %tok.1, bf16[8192,768]{1,0:T(8,128)(2,1)} %dout.1, bf16[8,768,768]{2,1,0:T(8,128)(2,1)} %w_ref.1, f32[8,768,768]{2,1,0:T(8,128)} %ainv.1), custom_call_target="tpu_custom_call" | custom-call | flops 318901321728 | bytes 209715200 | tf_op jit(solution)/shard_map/kfac_stack/pallas_call | solution.py:370
  532.6 57.4 %kfac_finish.1 = (f32[8,768,768]{2,1,0:T(8,128)}, f32[8,768,768]{2,1,0:T(8,128)}, f32[8,768,768]{2,1,0:T(8,128)}) custom-call(f32[8,8,48,768]{3,2,1,0:T(8,128)} %get-tuple-element.7.a_ref, f32[8,8,144,768]{3,2,1,0:T(8,128)} %get-tuple-element.8.g_ref, f32[8,8,768]{2,1,0:T(8,128)} %get-tuple-element.9.ax_ref, f32[8,8,768]{2,1,0:T(8,128)} %get-tuple-element.10.gx_ref, ...), custom_call_target="tpu_custom_call" | custom-call | flops 43486543872 | bytes 167772160 | tf_op jit(solution)/shard_map/kfac_finish/pallas_call | solution.py:467

commit v6 on v5

--- a/solution.py
+++ b/solution.py
@@ -12,14 +12,14 @@
 D = 768
 B = 256
 H = 128
-NT = 8
+NT = 4
 DEV = 8
 AR = 48
 GR = 96
 SR = AR + GR
 L = 8
 MESH = pl.DeviceIdType.MESH
-T1, T2, T3, T4, T5, T6, T7 = 0, 1, 0, 4, 2, 2, 4
+T1, T2, T3, T4, T5, T6, T7 = 0, 1, 3, 0, 3, 2, 3
 
 
 def tn(left, right):
@@ -136,7 +136,7 @@
         return pltpu.make_async_remote_copy(src_ref=src, dst_ref=dst, send_sem=ssem.at[p, k], recv_sem=rsem.at[p, k],
                                             device_id=dev, device_id_type=MESH)
 
-    def stages(rows, out, xout, idx2, idx3, idx4, bwd):
+    def stages(rows, out, xout, idx2, idx3, bwd):
         hh = rows // 2
 
         def c1(p, q):
@@ -195,12 +195,12 @@
             start(c2(p1, q1))
 
         def reduce3():
-            wait(c2(p2, q2))
-            ex[q2] += exr[p2, 1]
+            wait(c2(p1, q1))
+            ex[q1] += exr[p1, 1]
             for i in range(2):
-                acc[q2, chunk(i, cx, cc), 0:hh, :] += r2a[p2, i, 0:hh, :]
-                acc[q2, chunk(cy, i, cc), hh:rows, :] += r2b[p2, i, 0:hh, :]
-            start(c3(p2, q2))
+                acc[q1, chunk(i, cx, cc), 0:hh, :] += r2a[p1, i, 0:hh, :]
+                acc[q1, chunk(cy, i, cc), hh:rows, :] += r2b[p1, i, 0:hh, :]
+            start(c3(p1, q1))
 
         def reduce4():
             wait(c3(p2, q2))
@@ -224,36 +224,36 @@
             start(c4(p2, idx2))
 
         def gather5():
-            keep(p3, idx3).wait()
-            keep_x(p3, q3, idx3).wait()
-            wait(c4(p3, idx3))
-            start(c5(p3, idx3))
+            keep(p2, idx2).wait()
+            keep_x(p2, q2, idx2).wait()
+            wait(c4(p2, idx2))
+            start(c5(p2, idx2))
 
         def gather6():
-            wait(c5(p4, idx4))
-            start(c6(p4, idx4))
+            wait(c5(p3, idx3))
+            start(c6(p3, idx3))
 
         def gather7():
-            wait(c6(p4, idx4))
+            wait(c6(p3, idx3))
 
         return reduce1, reduce2, reduce3, reduce4, gather5, gather6, gather7
 
     def at(cond, step, fn):
         pl.when(cond & (t == step))(fn)
 
-    j1, j2, j3, j4 = w - 1, w - 2, w - 3, w - 4
-    p1, p2, p3, p4 = lax.rem(w + 1, 2), lax.rem(w, 2), lax.rem(w + 1, 2), lax.rem(w, 2)
-    q1, q2, q3 = lax.rem(w + 2, 3), lax.rem(w + 1, 3), lax.rem(w, 3)
-    fw = stages(AR, a_out, ax_out, j2, j3, j4, False)
-    bw = stages(SR, g_out, gx_out, j2 - L, j3 - L, j4 - L, True)
-    is_f = [(j >= 0) & (j < L) for j in (j1, j2, j3, j4)]
-    is_b = [(j >= L) & (j < 2 * L) for j in (j1, j2, j3, j4)]
-
-    @pl.when(is_b[1] & (t == 0))
-    def _():
-        pltpu.make_async_copy(ainv.at[L - 1 - (j2 - L)], ainv_v, asem).start()
-
-    for k, step, i in ((0, T1, 0), (2, T3, 1), (1, T2, 0), (5, T6, 3), (4, T5, 2), (3, T4, 1), (6, T7, 3)):
+    j1, j2, j3 = w - 1, w - 2, w - 3
+    p1, p2, p3 = lax.rem(w + 1, 2), lax.rem(w, 2), lax.rem(w + 1, 2)
+    q1, q2 = lax.rem(w + 2, 3), lax.rem(w + 1, 3)
+    fw = stages(AR, a_out, ax_out, j2, j3, False)
+    bw = stages(SR, g_out, gx_out, j2 - L, j3 - L, True)
+    is_f = [(j >= 0) & (j < L) for j in (j1, j2, j3)]
+    is_b = [(j >= L) & (j < 2 * L) for j in (j1, j2, j3)]
+
+    @pl.when(is_b[0] & (t == 2))
+    def _():
+        pltpu.make_async_copy(ainv.at[L - 1 - (j1 - L)], ainv_v, asem).start()
+
+    for k, step, i in ((0, T1, 0), (3, T4, 1), (1, T2, 0), (5, T6, 2), (2, T3, 0), (4, T5, 1), (6, T7, 2)):
         at(is_f[i], step, fw[k])
         at(is_b[i], step, bw[k])
 
@@ -369,7 +369,7 @@
 
     return pl.pallas_call(
         functools.partial(step_kernel, tile, inv_total),
-        grid=(2 * L + 4, NT),
+        grid=(2 * L + 3, NT),
         in_specs=[any_spec, any_spec, pl.BlockSpec((1, d, d), w_map), any_spec],
         out_specs=[any_spec] * 5,
         out_shape=[

time: 590 us -> 565 us (0.958)
  Pallas kernels: 589 us -> 564 us
    pallas_call x1, Pallas kernels: 532 us -> 507 us  [run_stack(): pl.pallas_call(functools.partial(step_kernel, tile, inv_total), grid=(2 *...]
where the time goes in v6:
time: 565 us
  Pallas kernels  564 us (100%)
    pallas_call x1, Pallas kernels, run_stack(): pl.pallas_call(functools.partial(step_kernel, tile, inv_total), grid=(2 *...  507 us
    pallas_call x1, Pallas kernels, finish(): pl.pallas_call(finish_kernel, grid=(L,), in_specs=[pl.BlockSpec((1, DEV,...  57.2 us

profile of v6, /device:TPU:0, one launch (start us, length us, event | category | flops | bytes accessed | tf_op | source)
XLA Modules:
  0.0 564.9 jit_solution(11953585308612128434)
XLA Ops:
  0.6 507.0 %kfac_stack.1 = (bf16[7,8192,768]{2,1,0:T(8,128)(2,1)}, f32[8,8,48,768]{3,2,1,0:T(8,128)}, f32[8,8,144,768]{3,2,1,0:T(8,128)}, f32[8,8,768]{2,1,0:T(8,128)}, f32[8,8,768]{2,1,0:T(8,128)}) custom-call(bf16[8192,768]{1,0:T(8,128)(2,1)} %tok.1, bf16[8192,768]{1,0:T(8,128)(2,1)} %dout.1, bf16[8,768,768]{2,1,0:T(8,128)(2,1)} %w_ref.1, f32[8,768,768]{2,1,0:T(8,128)} %ainv.1), custom_call_target="tpu_custom_call" | custom-call | flops 318901321728 | bytes 209715200 | tf_op jit(solution)/shard_map/kfac_stack/pallas_call | solution.py:370
  507.7 57.2 %kfac_finish.1 = (f32[8,768,768]{2,1,0:T(8,128)}, f32[8,768,768]{2,1,0:T(8,128)}, f32[8,768,768]{2,1,0:T(8,128)}) custom-call(f32[8,8,48,768]{3,2,1,0:T(8,128)} %get-tuple-element.7.a_ref, f32[8,8,144,768]{3,2,1,0:T(8,128)} %get-tuple-element.8.g_ref, f32[8,8,768]{2,1,0:T(8,128)} %get-tuple-element.9.ax_ref, f32[8,8,768]{2,1,0:T(8,128)} %get-tuple-element.10.gx_ref, ...), custom_call_target="tpu_custom_call" | custom-call | flops 43486543872 | bytes 167772160 | tf_op jit(solution)/shard_map/kfac_finish/pallas_call | solution.py:467
